TPU v7x, 32 devices: a whole 2x2x4 slice. The times are simulated.
32 devices in a mesh: gx: 8 (over z, y), gy: 4 (over x, core).
Axes of the slice: x: 2, y: 2, z: 4, core: 2. Of those that a mesh axis runs over, the one named last changes fastest.
Arguments:
- velocity: bfloat16 [3, 16, 16, 16, 512], P(None, 'gx', 'gy'), may hold values from -6 to 6
- part_pos: float32 [4096, 3, 128], P(('gx', 'gy')), may hold values from -1 to 1
- part_vel: float32 [4096, 3, 128], P(('gx', 'gy')), may hold values from -6 to 6
- part_coef: float32 [4096, 2, 128], P(('gx', 'gy')), may hold values from 0.3 to 3
- counts: int32 [4096], P(('gx', 'gy')), may hold values from 1 to 128
- dest: int32 [4096], P(('gx', 'gy')), may hold values from 0 to 3, as said below
- elem: int32 [4096], P(('gx', 'gy')), may hold values from 0 to 127, as said below
Outputs:
- drag: float32 [4096, 3, 128], P(('gx', 'gy'))
- source: float32 [3, 16, 16, 16, 512], P(None, 'gx', 'gy')
Inputs may be any that keep to these rules, and one draw needn't show every extreme that they name: `dest`: every device sends exactly 32 blocks to each gy index. `elem`: on every owning device, each of its 128 elements receives exactly one block.
All inputs are finite; a program needn't handle non-finite values.
Results may differ from a plain program's by a relative error of at most 0.0003.
Values sent between devices are 32-bit elements; how exact they have to be, the bound alone decides.
A program may use at most 128 MiB of HBM per device.

v0:
```python
import functools

import jax
import jax.numpy as jnp
from jax import lax
from jax.experimental import pallas as pl
from jax.experimental.pallas import tpu as pltpu
from jax.sharding import PartitionSpec as P

GLL = (
    -1.0,
    -0.8717401485096066,
    -0.5917001814331423,
    -0.2092992179024789,
    0.2092992179024789,
    0.5917001814331423,
    0.8717401485096066,
    1.0,
)
SHARPNESS = 8.0
VMEM = pltpu.VMEM
SMEM = pltpu.SMEM
ROWS = 24


def lane_iota(shape):
    return lax.broadcasted_iota(jnp.int32, shape, len(shape) - 1)


def node_consts():
    row = lax.broadcasted_iota(jnp.int32, (8, 128), 0)

    def pick(values):
        out = jnp.full((8, 128), values[7], jnp.float32)
        for i in range(7):
            out = jnp.where(row == i, jnp.float32(values[i]), out)
        return out

    others = [pick([[GLL[m] for m in range(8) if m != i][n] for i in range(8)]) for n in range(7)]
    scales = []
    for i in range(8):
        product = 1.0
        for m in range(8):
            if m != i:
                product *= GLL[i] - GLL[m]
        scales.append(1.0 / product)
    return pick(GLL), others, pick(scales)


def lagrange(x, others, scale):
    diffs = [x - o for o in others]
    left = (diffs[0] * diffs[1]) * (diffs[2] * diffs[3])
    right = (diffs[4] * diffs[5]) * (diffs[6] * scale)
    return left * right


def gauss(x, nodes):
    gap = nodes - x
    return jnp.exp(-SHARPNESS * gap * gap)


def split(x):
    high = x.astype(jnp.bfloat16)
    low = (x - high.astype(jnp.float32)).astype(jnp.bfloat16)
    return high, low


def planes(a, b):
    return jnp.concatenate([a[j : j + 1] * b for j in range(8)], axis=0)


def spread_nodes(vel_ref, vs_ref, elems):
    low = lane_iota((elems, 128)) < 64
    for c in range(3):
        for q in range(4):
            x = vel_ref[c, :, q * 128 : (q + 1) * 128].astype(jnp.float32)
            turned = pltpu.roll(x, 64, 1)
            vs_ref[pl.ds(c * 8 + 2 * q, elems, stride=ROWS), :] = jnp.where(low, x, turned)
            vs_ref[pl.ds(c * 8 + 2 * q + 1, elems, stride=ROWS), :] = jnp.where(low, turned, x)


def st_planes(s, t, nodes):
    high, low = split(planes(gauss(s, nodes), gauss(t, nodes)))
    gathered = jnp.concatenate([high, low], axis=0)
    return jnp.concatenate([gathered, gathered], axis=1)


def project(left, gathered):
    high, low = split(left)
    return lax.dot_general(
        jnp.concatenate([high, low], axis=1),
        gathered,
        (((1,), (1,)), ((), ())),
        preferred_element_type=jnp.float32,
    )


def element(block, count, field, consts, inner_minus, inner_plus):
    nodes, others, scale = consts
    r, s, t = (jnp.broadcast_to(block[d : d + 1], (8, 128)) for d in range(3))
    basis_r = lagrange(r, others, scale)
    basis_st = planes(lagrange(s, others, scale), lagrange(t, others, scale))
    high, low = split(basis_st)
    partial = jnp.dot(
        field.astype(jnp.bfloat16),
        jnp.concatenate([high, low], axis=0),
        preferred_element_type=jnp.float32,
    )
    rel = []
    for c in range(3):
        fluid = jnp.sum(partial[c * 8 : c * 8 + 8] * basis_r, axis=0, keepdims=True)
        rel.append(fluid - block[3 + c : 4 + c])
    speed = jnp.sqrt(rel[0] * rel[0] + rel[1] * rel[1] + rel[2] * rel[2])
    power = jnp.exp(0.687 * jnp.log(block[7:8] * speed))
    factor = block[6:7] * (1.0 + 0.15 * power)
    factor = jnp.where(lane_iota((1, 128)) < count, factor, 0.0)
    drag = [factor * w for w in rel]
    whole = jnp.concatenate(drag, axis=0)
    minus = gauss(r + 2.0, nodes)
    plus = gauss(r - 2.0, nodes)
    weights = [gauss(r, nodes)]
    if inner_minus:
        weights.append(minus)
    if inner_plus:
        weights.append(plus)
    rows = [(-d) * w for w in weights for d in drag]
    blank = jnp.zeros((5, 128), jnp.float32)
    if not inner_minus:
        rows.append(jnp.concatenate([-whole * minus[7:8], blank], axis=0))
    if not inner_plus:
        rows.append(jnp.concatenate([-whole * plus[0:1], blank], axis=0))
    out = project(jnp.concatenate(rows, axis=0), st_planes(s, t, nodes))
    parts, at = {}, ROWS
    parts["own"] = out[0:ROWS]
    for name, inner in (("minus", inner_minus), ("plus", inner_plus)):
        if inner:
            parts[name] = out[at : at + ROWS]
            at += ROWS
    for name, inner in (("minus", inner_minus), ("plus", inner_plus)):
        if not inner:
            parts[name] = out[at : at + 8]
            at += 8
    return whole, parts


def main_kernel(
    shape, chunks, n_gx, n_gy,
    slot_ref, count_ref, elem_ref, got_ref, vel_ref,
    field_ref, far_lo_ref, far_hi_ref, ret_ref,
    vs_ref, ts_ref, fs_ref, drag_ref, pos_ref, gpos_ref, gdrag_ref,
    face_ref, gface_ref, lo_ref, hi_ref, back_ref,
    pos_sem, drag_sem, face_sem, y_sem, back_sem,
):
    exd, eyd, ez = shape
    elems = exd * eyd * ez
    columns = eyd * ez
    share = elems // n_gy
    wide = columns // chunks
    group = min(8, wide)
    turns = columns // group
    per = turns // chunks
    half = columns // 2
    gx = lax.axis_index("gx")
    gy = lax.axis_index("gy")
    has = (gx > 0, gx < n_gx - 1)
    mesh_id = pl.DeviceIdType.MESH

    def to_side(side, src, dst, sems, *at):
        return pltpu.make_async_remote_copy(
            src_ref=src, dst_ref=dst,
            send_sem=sems.at[(0, side) + at], recv_sem=sems.at[(1, 1 - side) + at],
            device_id={"gx": gx - 1 if side == 0 else gx + 1}, device_id_type=mesh_id,
        )

    def from_side(side, src, dst, sems, *at):
        return pltpu.make_async_remote_copy(
            src_ref=src, dst_ref=dst,
            send_sem=sems.at[(0, side) + at], recv_sem=sems.at[(1, side) + at],
            device_id={"gx": gx - 1 if side == 0 else gx + 1}, device_id_type=mesh_id,
        )

    barrier = pltpu.get_barrier_semaphore()
    for side in range(2):
        @pl.when(has[side])
        def _():
            pl.semaphore_signal(
                barrier, inc=1, device_id={"gx": gx - 1 if side == 0 else gx + 1}, device_id_type=mesh_id
            )
    for off in range(1, n_gy):
        pl.semaphore_signal(
            barrier, inc=1, device_id={"gy": lax.rem(gy + off, n_gy)}, device_id_type=mesh_id
        )

    base = (0, elems - columns)

    def stage(index, carry):
        spots = [(side, index * 4 + u) for side in range(2) for u in range(4)]
        held = [got_ref[slot_ref[base[side] + col], 0:3] for side, col in spots]
        for (side, col), value in zip(spots, held):
            pos_ref[side, col] = value
        return carry

    lax.fori_loop(0, columns // 4, stage, 0)
    pl.semaphore_wait(
        barrier, n_gy - 1 + (gx > 0).astype(jnp.int32) + (gx < n_gx - 1).astype(jnp.int32)
    )
    for side in range(2):
        @pl.when(has[side])
        def _():
            to_side(side, pos_ref.at[side], gpos_ref.at[1 - side], pos_sem).start()

    spread_nodes(vel_ref, vs_ref, elems)
    consts = node_consts()
    nodes = consts[0]

    def drag_copy(make, side, chunk):
        start = base[side] + chunk * wide
        return make(
            side, drag_ref.at[pl.ds(start, wide)], gdrag_ref.at[1 - side, pl.ds(chunk * wide, wide)], drag_sem, chunk
        )

    def turn(index, carry):
        for g in range(group):
            col = index * group + g
            parts = []
            for x in range(exd):
                e = x * columns + col
                slot = slot_ref[e]
                drag, part = element(
                    got_ref[slot],
                    count_ref[slot],
                    vs_ref[pl.ds(pl.multiple_of(e * ROWS, 8), ROWS), :],
                    consts,
                    x > 0,
                    x + 1 < exd,
                )
                drag_ref[e] = drag
                parts.append(part)
            for x in range(exd):
                e = x * columns + col
                own = parts[x]["own"]
                if x + 1 < exd:
                    own = own + parts[x + 1]["minus"]
                if x > 0:
                    own = own + parts[x - 1]["plus"]
                ts_ref[pl.ds(pl.multiple_of(e * ROWS, 8), ROWS), :] = own
            start = pl.multiple_of(col * 8, 8)
            fs_ref[0, pl.ds(start, 8), :] = parts[0]["minus"]
            fs_ref[1, pl.ds(start, 8), :] = parts[exd - 1]["plus"]
        for side in range(2):
            @pl.when((lax.rem(index, per) == per - 1) & has[side])
            def _():
                drag_copy(to_side, side, lax.div(index, per)).start()
        return carry

    lax.fori_loop(0, turns, turn, 0)

    def doubled(x):
        return x + pltpu.roll(x, 64, 1)

    low_h = lane_iota((half, 128)) < 64
    for side in range(2):
        node = 0 if side == 0 else 7
        for c in range(3):
            one = doubled(ts_ref[pl.ds(base[side] * ROWS + c * 8 + node, half, stride=ROWS), :])
            two = doubled(ts_ref[pl.ds((base[side] + half) * ROWS + c * 8 + node, half, stride=ROWS), :])
            face_ref[side, c] = jnp.where(low_h, one, two)
        @pl.when(has[side])
        def _():
            to_side(side, face_ref.at[side], gface_ref.at[1 - side], face_sem).start()

    def fill(index, carry):
        held = [drag_ref[elem_ref[index * 8 + u]] for u in range(8)]
        for u in range(8):
            back_ref[index * 8 + u] = held[u]
        return carry

    lax.fori_loop(0, elems // 8, fill, 0)

    def back_copy(off):
        peer = lax.rem(gy + off, n_gy)
        return pltpu.make_async_remote_copy(
            src_ref=back_ref.at[pl.ds(peer * share, share)], dst_ref=ret_ref.at[pl.ds(gy * share, share)],
            send_sem=back_sem.at[0, off - 1], recv_sem=back_sem.at[1, off - 1],
            device_id={"gy": peer}, device_id_type=mesh_id,
        )

    for off in range(1, n_gy):
        back_copy(off).start()

    mine = pl.ds(gy * share, share)
    ret_ref[mine] = back_ref[mine]

    for side in range(2):
        @pl.when(has[side])
        def _():
            from_side(side, pos_ref.at[side], gpos_ref.at[side], pos_sem).wait()

        def ghost(chunk, carry):
            from_side(
                side, drag_ref.at[pl.ds(base[side] + chunk * wide, wide)],
                gdrag_ref.at[side, pl.ds(chunk * wide, wide)], drag_sem, chunk,
            ).wait()
            sums = []
            for g in range(wide):
                col = chunk * wide + g
                place = gpos_ref[side, col]
                force = gdrag_ref[side, col]
                r, s, t = (jnp.broadcast_to(place[d : d + 1], (8, 128)) for d in range(3))
                weight = gauss(r + (-2.0 if side == 0 else 2.0), nodes)
                rows = [(-force[c : c + 1]) * weight for c in range(3)]
                add = project(jnp.concatenate(rows, axis=0), st_planes(s, t, nodes))
                spot = pl.ds(pl.multiple_of((base[side] + col) * ROWS, 8), ROWS)
                sums.append((spot, ts_ref[spot, :] + add))
            for spot, value in sums:
                ts_ref[spot, :] = value
            return carry

        @pl.when(has[side])
        def _():
            lax.fori_loop(0, chunks, ghost, 0)

    for side in range(2):
        @pl.when(has[side])
        def _():
            from_side(side, face_ref.at[side], gface_ref.at[side], face_sem).wait()

    low = lane_iota((ez, 128)) < 64
    spot64 = lane_iota((ez, 128)) % 64

    def lanes(c, x, y, q):
        start = ((x * eyd + y) * ez) * ROWS + c * 8 + 2 * q
        even = ts_ref[pl.ds(start, ez, stride=ROWS), :]
        odd = ts_ref[pl.ds(start + 1, ez, stride=ROWS), :]
        return jnp.where(low, even, odd) + pltpu.roll(jnp.where(low, odd, even), 64, 1)

    def far(side, c, y):
        col = y * ez
        upper = col >= half
        row = col - half if upper else col
        came = gface_ref[side, c, row : row + ez, :]
        turned = pltpu.roll(came, 64, 1)
        came = jnp.where(low, turned, came) if upper else jnp.where(low, came, turned)
        mine = doubled(fs_ref[side, pl.ds(col * 8 + c, ez, stride=8), :])
        return jnp.where(has[side], came + mine, 0.0)

    for y in (0, eyd - 1) + tuple(range(1, eyd - 1)):
        for c in range(3):
            grid = [[lanes(c, x, y, q) for q in range(4)] for x in range(exd)]
            for x in range(exd):
                above = pltpu.roll(grid[x + 1][0], 64, 1) if x + 1 < exd else far(1, c, y)
                below = pltpu.roll(grid[x - 1][3], 64, 1) if x > 0 else far(0, c, y)
                done = list(grid[x])
                done[3] = done[3] + jnp.where(low, 0.0, above)
                done[0] = done[0] + jnp.where(low, below, 0.0)
                for q in range(4):
                    field_ref[c, x, y, :, q * 128 : (q + 1) * 128] = done[q]
                if y == 0:
                    face = jnp.where(spot64 < 8, done[0], 0.0)
                    for q in range(1, 4):
                        face = face + pltpu.roll(jnp.where(spot64 < 8, done[q], 0.0), 8 * q, 1)
                    lo_ref[c, x] = face
                if y == eyd - 1:
                    face = jnp.where(spot64 >= 56, done[0], 0.0)
                    for q in range(1, 4):
                        face = face + pltpu.roll(jnp.where(spot64 >= 56, done[q], 0.0), 128 - 8 * q, 1)
                    hi_ref[c, x] = face
        if y == eyd - 1:
            lo_copy = pltpu.make_async_remote_copy(
                src_ref=lo_ref, dst_ref=far_lo_ref, send_sem=y_sem.at[0, 0], recv_sem=y_sem.at[1, 0],
                device_id={"gy": gy - 1}, device_id_type=mesh_id,
            )
            hi_copy = pltpu.make_async_remote_copy(
                src_ref=hi_ref, dst_ref=far_hi_ref, send_sem=y_sem.at[0, 1], recv_sem=y_sem.at[1, 1],
                device_id={"gy": gy + 1}, device_id_type=mesh_id,
            )
            @pl.when(gy > 0)
            def _():
                lo_copy.start()
            @pl.when(gy < n_gy - 1)
            def _():
                hi_copy.start()

    @pl.when(gy > 0)
    def _():
        lo_copy.wait_send()
        hi_copy.wait_recv()
    @pl.when(gy < n_gy - 1)
    def _():
        hi_copy.wait_send()
        lo_copy.wait_recv()
    for off in range(1, n_gy):
        back_copy(off).wait()


def run_main(slot, count, elem_of, got, velocity, shape):
    exd, eyd, ez = shape
    elems = exd * eyd * ez
    columns = eyd * ez
    n_gx, n_gy = lax.axis_size("gx"), lax.axis_size("gy")
    chunks = 4
    f32 = jnp.float32
    dma = pltpu.SemaphoreType.DMA
    face = (3, exd, ez, 128)
    return pl.pallas_call(
        functools.partial(main_kernel, shape, chunks, n_gx, n_gy),
        out_shape=(
            jax.ShapeDtypeStruct((3, exd, eyd, ez, 512), f32),
            jax.ShapeDtypeStruct(face, f32),
            jax.ShapeDtypeStruct(face, f32),
            jax.ShapeDtypeStruct((elems, 3, 128), f32),
        ),
        in_specs=[pl.BlockSpec(memory_space=SMEM)] * 3 + [pl.BlockSpec(memory_space=VMEM)] * 2,
        out_specs=[pl.BlockSpec(memory_space=VMEM)] * 4,
        scratch_shapes=[
            pltpu.VMEM((elems * ROWS, 128), f32),
            pltpu.VMEM((elems * ROWS, 128), f32),
            pltpu.VMEM((2, columns * 8, 128), f32),
            pltpu.VMEM((elems, 3, 128), f32),
            pltpu.VMEM((2, columns, 3, 128), f32),
            pltpu.VMEM((2, columns, 3, 128), f32),
            pltpu.VMEM((2, columns, 3, 128), f32),
            pltpu.VMEM((2, 3, columns // 2, 128), f32),
            pltpu.VMEM((2, 3, columns // 2, 128), f32),
            pltpu.VMEM(face, f32),
            pltpu.VMEM(face, f32),
            pltpu.VMEM((elems, 3, 128), f32),
            dma((2, 2)),
            dma((2, 2, chunks)),
            dma((2, 2)),
            dma((2, 2)),
            dma((2, n_gy - 1)),
        ],
        compiler_params=pltpu.CompilerParams(
            vmem_limit_bytes=48 * 1024 * 1024, collective_id=0, has_side_effects=True
        ),
        cost_estimate=pl.CostEstimate(flops=200_000_000, bytes_accessed=4_000_000, transcendentals=700_000),
        name="elements",
    )(slot, count, elem_of, got, velocity)


def yz_pass(position_ref, field_ref, far_lo_ref, far_hi_ref, ret_ref, out_ref, drag_ref, buf_ref, sem):
    _, exd, eyd, ez, _ = field_ref.shape
    at = lax.axis_index("gy")
    first = at > 0
    last = at < lax.axis_size("gy") - 1
    place = lane_iota((ez, 128)) % 64
    k = lane_iota((ez, 128)) % 8
    row = lax.broadcasted_iota(jnp.int32, (ez, 128), 0)
    up = (k == 7) & (row < ez - 1)
    down = (k == 0) & (row > 0)
    copies = []
    for c in range(3):
        for x in range(exd):
            far_lo = jnp.where(last, far_lo_ref[c, x], 0.0)
            far_hi = jnp.where(first, far_hi_ref[c, x], 0.0)
            for q in range(4):
                spot = slice(q * 128, (q + 1) * 128)
                cells = [field_ref[c, x, y, :, spot] for y in range(eyd)]
                for y in range(eyd):
                    if y + 1 < eyd:
                        above = pltpu.roll(cells[y + 1], 56, 1)
                    else:
                        above = pltpu.roll(far_lo, (56 - 8 * q) % 128, 1)
                    if y > 0:
                        below = pltpu.roll(cells[y - 1], 72, 1)
                    else:
                        below = pltpu.roll(far_hi, (72 + 8 * q) % 128, 1)
                    v = cells[y] + jnp.where(place >= 56, above, 0.0) + jnp.where(place < 8, below, 0.0)
                    nxt = pltpu.roll(pltpu.roll(v, ez - 1, 0), 7, 1)
                    prv = pltpu.roll(pltpu.roll(v, 1, 0), 121, 1)
                    buf_ref[c, x, y, :, spot] = v + jnp.where(up, nxt, 0.0) + jnp.where(down, prv, 0.0)


            copies.append(pltpu.make_async_copy(buf_ref.at[c, x], out_ref.at[c, x], sem.at[c, x]))
            copies[-1].start()

    def pick(index, carry):
        held = [ret_ref[position_ref[index * 8 + u]] for u in range(8)]
        for c in range(3):
            rows = jnp.concatenate([h[c : c + 1] for h in held], axis=0)
            drag_ref[c, pl.ds(pl.multiple_of(index * 8, 8), 8), :] = rows
        return carry

    lax.fori_loop(0, ret_ref.shape[0] // 8, pick, 0)
    for copy in copies:
        copy.wait()


def run_yz(position, field, far_lo, far_hi, ret):
    f32 = jnp.float32
    return pl.pallas_call(
        yz_pass,
        out_shape=(jax.ShapeDtypeStruct(field.shape, f32), jax.ShapeDtypeStruct((3, ret.shape[0], 128), f32)),
        in_specs=[pl.BlockSpec(memory_space=SMEM)] + [pl.BlockSpec(memory_space=VMEM)] * 4,
        out_specs=[pl.BlockSpec(memory_space=pl.ANY), pl.BlockSpec(memory_space=VMEM)],
        scratch_shapes=[pltpu.VMEM(field.shape, f32), pltpu.SemaphoreType.DMA(field.shape[:2])],
        compiler_params=pltpu.CompilerParams(vmem_limit_bytes=32 * 1024 * 1024),
        name="yzpass",
    )(position, field, far_lo, far_hi, ret)


def send_kernel(
    n_gy, sorting_ref, pos_ref, vel_ref, coef_ref, label_ref,
    got_ref, got_label_ref, send_ref, sem, label_sem,
):
    share = pos_ref.shape[1] // n_gy
    gy = lax.axis_index("gy")
    mesh_id = pl.DeviceIdType.MESH
    barrier = pltpu.get_barrier_semaphore()
    for off in range(1, n_gy):
        pl.semaphore_signal(
            barrier, inc=1, device_id={"gy": lax.rem(gy + off, n_gy)}, device_id_type=mesh_id
        )

    def block_copy(off):
        peer = lax.rem(gy + off, n_gy)
        return pltpu.make_async_remote_copy(
            src_ref=send_ref.at[pl.ds(peer * share, share)], dst_ref=got_ref.at[pl.ds(gy * share, share)],
            send_sem=sem.at[0, off - 1], recv_sem=sem.at[1, off - 1],
            device_id={"gy": peer}, device_id_type=mesh_id,
        )

    def label_copy(off):
        peer = lax.rem(gy + off, n_gy)
        return pltpu.make_async_remote_copy(
            src_ref=label_ref.at[peer], dst_ref=got_label_ref.at[gy],
            send_sem=label_sem.at[0, off - 1], recv_sem=label_sem.at[1, off - 1],
            device_id={"gy": peer}, device_id_type=mesh_id,
        )

    def pack(dst, start):
        def some(index, carry):
            held = []
            for u in range(4):
                b = sorting_ref[start + index * 4 + u]
                rows = [ref[c, pl.ds(b, 1), :] for ref in (pos_ref, vel_ref) for c in range(3)]
                held.append(jnp.concatenate(rows + [coef_ref[b]], axis=0))
            for u in range(4):
                dst[start + index * 4 + u] = held[u]
            return carry

        lax.fori_loop(0, share // 4, some, 0)

    order = sorted(range(1, n_gy), key=lambda off: -min(off, n_gy - off))
    for place, off in enumerate(order):
        pack(send_ref, lax.rem(gy + off, n_gy) * share)
        if place == 0:
            pl.semaphore_wait(barrier, n_gy - 1)
            for other in order:
                label_copy(other).start()
        block_copy(off).start()
    pack(got_ref, gy * share)
    got_label_ref[gy] = label_ref[gy]
    for off in order:
        label_copy(off).wait()
    for off in order:
        block_copy(off).wait()


def run_send(sorting, pos, vel, coef, label):
    n_gy = lax.axis_size("gy")
    elems = pos.shape[1]
    f32 = jnp.float32
    dma = pltpu.SemaphoreType.DMA
    return pl.pallas_call(
        functools.partial(send_kernel, n_gy),
        out_shape=(
            jax.ShapeDtypeStruct((elems, 8, 128), f32),
            jax.ShapeDtypeStruct(label.shape, f32),
        ),
        in_specs=[pl.BlockSpec(memory_space=SMEM)] + [pl.BlockSpec(memory_space=VMEM)] * 4,
        out_specs=[pl.BlockSpec(memory_space=VMEM)] * 2,
        scratch_shapes=[
            pltpu.VMEM((elems, 8, 128), f32),
            dma((2, n_gy - 1)),
            dma((2, n_gy - 1)),
        ],
        compiler_params=pltpu.CompilerParams(
            vmem_limit_bytes=32 * 1024 * 1024, collective_id=1, has_side_effects=True
        ),
        name="migrate",
    )(sorting, pos, vel, coef, label)


def inverse_of(position):
    n = position.shape[0]
    ladder = jnp.arange(n, dtype=jnp.int32)
    return jnp.sum(jnp.where(position[None, :] == ladder[:, None], ladder[None, :], 0), axis=1)


def body(velocity, part_pos, part_vel, part_coef, counts, dest, elem):
    _, exd, eyd, ez, nodes = velocity.shape
    elems = exd * eyd * ez
    devices = lax.axis_size("gy")
    share = elems // devices
    f32 = jnp.float32
    ladder = jnp.arange(elems, dtype=jnp.int32)
    earlier = (dest[None, :] == dest[:, None]) & (ladder[None, :] < ladder[:, None])
    position = dest * share + jnp.sum(earlier.astype(jnp.int32), axis=1)
    sorting = inverse_of(position)
    lanes = max(128, share)
    tags = elem * 256 + counts
    room = (position // share) * lanes + position % share
    cells = jnp.arange(devices * lanes, dtype=jnp.int32)
    label = jnp.sum(jnp.where(room[None, :] == cells[:, None], tags[None, :], 0), axis=1)
    got, got_label = run_send(
        sorting, part_pos.transpose(1, 0, 2), part_vel.transpose(1, 0, 2), part_coef,
        label.astype(f32).reshape(devices, 1, lanes),
    )
    got_labels = got_label[:, 0, :share].reshape(elems).astype(jnp.int32)
    slot = inverse_of(got_labels // 256)
    field, far_lo, far_hi, ret = run_main(
        slot, got_labels % 256, got_labels // 256, got,
        velocity.reshape(3, elems, nodes), (exd, eyd, ez),
    )
    source, drag_out = run_yz(position, field, far_lo, far_hi, ret)
    return (drag_out.transpose(1, 0, 2), source)


def solution(mesh):
    in_specs = (
        P(None, "gx", "gy", None, None),
        P(("gx", "gy"), None, None),
        P(("gx", "gy"), None, None),
        P(("gx", "gy"), None, None),
        P(("gx", "gy")),
        P(("gx", "gy")),
        P(("gx", "gy")),
    )
    out_specs = (P(("gx", "gy"), None, None), P(None, "gx", "gy", None, None))
    return jax.shard_map(body, mesh=mesh, in_specs=in_specs, out_specs=out_specs, check_vma=False)
```

profile of v0, /device:TPU:9, one launch (start us, length us, event | category | flops | bytes accessed | tf_op | source)
XLA Modules:
  0.0 49.0 jit_solution(4923529894473801961)
XLA Ops:
  0.6 0.0 copy-start.4
  0.6 0.6 %copy-done.4 = s32[128]{0:T(128)S(1)} copy-done((s32[128]{0:T(128)S(1)}, s32[128]{0:T(128)}, u32[]{:S(2)}) %copy-start.4) | copy-done | bytes 536
  1.3 0.0 copy-start.5
  1.3 0.0 copy-start.6
  1.3 0.2 convert_reduce_fusion
  1.5 0.5 copy-done.5
  1.9 0.0 copy-done.6
  2.0 0.1 select_reduce_fusion.2.sorting_ref
  2.1 0.2 select_reduce_fusion
  2.2 0.0 copy-start
  2.3 0.9 %copy-done = f32[128,3,128]{2,0,1:T(8,128)S(1)} copy-done((f32[128,3,128]{2,0,1:T(8,128)S(1)}, f32[128,3,128]{2,0,1:T(8,128)}, u32[]{:S(2)}) %copy-start) | copy-done | bytes 196632
  3.2 0.0 copy-start.1
  3.2 0.9 %copy-done.1 = f32[128,3,128]{2,0,1:T(8,128)S(1)} copy-done((f32[128,3,128]{2,0,1:T(8,128)S(1)}, f32[128,3,128]{2,0,1:T(8,128)}, u32[]{:S(2)}) %copy-start.1) | copy-done | bytes 196632
  4.1 0.0 copy-start.2
  4.1 0.9 %copy-done.2 = f32[128,2,128]{2,1,0:T(2,128)S(1)} copy-done((f32[128,2,128]{2,1,0:T(2,128)S(1)}, f32[128,2,128]{2,1,0:T(2,128)}, u32[]{:S(2)}) %copy-start.2) | copy-done | bytes 131096
  5.0 0.0 copy-start.3
  5.0 9.3 %migrate.1 = (f32[128,8,128]{2,1,0:T(8,128)S(1)}, f32[4,1,128]{2,1,0:T(1,128)S(1)}) custom-call(s32[128]{0:T(128)S(1)} %select_reduce_fusion.2.sorting_ref, f32[3,128,128]{2,1,0:T(8,128)S(1)} %bitcast.5, f32[3,128,128]{2,1,0:T(8,128)S(1)} %bitcast.6, f32[128,2,128]{2,1,0:T(2,128)S(1)} %copy-done.2, f32[4,1,128]{2,1,0:T(1,128)S(1)} %bitcast.7), custom_call_target="tpu_custom_call" | custom-call | tf_op jit(solution)/shard_map/migrate/pallas_call | solution.py:566
  14.3 0.1 convert_element_type.30
  14.4 0.1 select_reduce_fusion.1.slot_ref
  14.5 0.0 copy-done.3
  14.5 26.3 %elements.1 = (f32[3,2,4,16,512]{4,3,2,1,0:T(8,128)S(1)}, f32[3,2,16,128]{3,2,1,0:T(8,128)S(1)}, f32[3,2,16,128]{3,2,1,0:T(8,128)S(1)}, f32[128,3,128]{2,1,0:T(4,128)S(1)}) custom-call(s32[128]{0:T(128)S(1)} %select_reduce_fusion.1.slot_ref, s32[128]{0:T(128)S(1)} %get-tuple-element.20.count_ref, s32[128]{0:T(128)S(1)} %get-tuple-element.21.elem_ref, ...), custom_call_target="tpu_custom_call" | custom-call | flops 200000000 | bytes 4000000 | tf_op jit(solution)/shard_map/elements/pallas_call | solution.py:405
  40.9 8.2 %yzpass.1 = (f32[3,2,4,16,512]{4,3,2,1,0:T(8,128)}, f32[3,128,128]{2,1,0:T(8,128)}) custom-call(s32[128]{0:T(128)S(1)} %get-tuple-element.19.position_ref, f32[3,2,4,16,512]{4,3,2,1,0:T(8,128)S(1)} %get-tuple-element.12.field_ref, f32[3,2,16,128]{3,2,1,0:T(8,128)S(1)} %get-tuple-element.13.far_lo_ref, f32[3,2,16,128]{3,2,1,0:T(8,128)S(1)} %get-tuple-element.14.far_hi_ref, ...), custom_call_target="tpu_custom_call" | custom-call | tf_op jit(solution)/shard_map/yzpass/pallas_call | solution.py:492
  (4 shorter events, 0.1 us)
Async XLA Ops:
  0.6 0.7 %copy-start.4 = (s32[128]{0:T(128)S(1)}, s32[128]{0:T(128)}, u32[]{:S(2)}) copy-start(s32[128]{0:T(128)} %param.12) | copy-start | bytes 1540
  1.3 0.7 %copy-start.5 = (s32[128]{0:T(128)S(1)}, s32[128]{0:T(128)}, u32[]{:S(2)}) copy-start(s32[128]{0:T(128)} %param.11) | copy-start | bytes 1540
  1.3 0.7 %copy-start.6 = (s32[128]{0:T(128)S(1)}, s32[128]{0:T(128)}, u32[]{:S(2)}) copy-start(s32[128]{0:T(128)} %param.13) | copy-start | bytes 1540
  2.2 0.9 %copy-start = (f32[128,3,128]{2,0,1:T(8,128)S(1)}, f32[128,3,128]{2,0,1:T(8,128)}, u32[]{:S(2)}) copy-start(f32[128,3,128]{2,0,1:T(8,128)} %param.8) | copy-start | bytes 589828
  3.2 0.9 %copy-start.1 = (f32[128,3,128]{2,0,1:T(8,128)S(1)}, f32[128,3,128]{2,0,1:T(8,128)}, u32[]{:S(2)}) copy-start(f32[128,3,128]{2,0,1:T(8,128)} %param.9) | copy-start | bytes 589828
  4.1 0.9 %copy-start.2 = (f32[128,2,128]{2,1,0:T(2,128)S(1)}, f32[128,2,128]{2,1,0:T(2,128)}, u32[]{:S(2)}) copy-start(f32[128,2,128]{2,1,0:T(2,128)} %coef_ref.1) | copy-start | bytes 393220
  5.0 9.5 %copy-start.3 = (bf16[3,2,4,16,512]{4,3,2,1,0:T(8,128)(2,1)S(1)}, bf16[3,2,4,16,512]{4,3,2,1,0:T(8,128)(2,1)}, u32[]{:S(2)}) copy-start(bf16[3,2,4,16,512]{4,3,2,1,0:T(8,128)(2,1)} %param.7) | copy-start | bytes 1179652
where the time goes:
time: 49.2 us; the launch traced here: 49 us
  Pallas kernels  43.8 us (89%)
  local copies, waits for them, and re-layouts  3.98 us (8%)
  between operations  0.7 us (1%)
  other arithmetic  0.59 us (1%)
    pallas_call x1, Pallas kernels, run_main(): pl.pallas_call(functools.partial(main_kernel, shape, chunks, n_gx, n_gy),...  26.3 us
    pallas_call x1, Pallas kernels, run_send(): pl.pallas_call(functools.partial(send_kernel, n_gy), out_shape=(jax.Shape...  9.29 us
    pallas_call x1, Pallas kernels, run_yz(): pl.pallas_call(yz_pass, out_shape=(jax.ShapeDtypeStruct(field.shape, f32)...  8.17 us
    unnamed x14, local copies, waits for them, and re-layouts  3.9 us

commit v1 on v0

--- a/solution.py
+++ b/solution.py
@@ -449,31 +449,34 @@
     row = lax.broadcasted_iota(jnp.int32, (ez, 128), 0)
     up = (k == 7) & (row < ez - 1)
     down = (k == 0) & (row > 0)
-    copies = []
-    for c in range(3):
-        for x in range(exd):
-            far_lo = jnp.where(last, far_lo_ref[c, x], 0.0)
-            far_hi = jnp.where(first, far_hi_ref[c, x], 0.0)
-            for q in range(4):
-                spot = slice(q * 128, (q + 1) * 128)
-                cells = [field_ref[c, x, y, :, spot] for y in range(eyd)]
-                for y in range(eyd):
-                    if y + 1 < eyd:
-                        above = pltpu.roll(cells[y + 1], 56, 1)
-                    else:
-                        above = pltpu.roll(far_lo, (56 - 8 * q) % 128, 1)
-                    if y > 0:
-                        below = pltpu.roll(cells[y - 1], 72, 1)
-                    else:
-                        below = pltpu.roll(far_hi, (72 + 8 * q) % 128, 1)
-                    v = cells[y] + jnp.where(place >= 56, above, 0.0) + jnp.where(place < 8, below, 0.0)
-                    nxt = pltpu.roll(pltpu.roll(v, ez - 1, 0), 7, 1)
-                    prv = pltpu.roll(pltpu.roll(v, 1, 0), 121, 1)
-                    buf_ref[c, x, y, :, spot] = v + jnp.where(up, nxt, 0.0) + jnp.where(down, prv, 0.0)
-
-
-            copies.append(pltpu.make_async_copy(buf_ref.at[c, x], out_ref.at[c, x], sem.at[c, x]))
-            copies[-1].start()
+
+    def out_copy(c, x):
+        return pltpu.make_async_copy(buf_ref.at[c, x], out_ref.at[c, x], sem.at[c, x])
+
+    def layer(index, carry):
+        c, x = lax.div(index, exd), lax.rem(index, exd)
+        far_lo = jnp.where(last, far_lo_ref[c, x], 0.0)
+        far_hi = jnp.where(first, far_hi_ref[c, x], 0.0)
+        for q in range(4):
+            spot = slice(q * 128, (q + 1) * 128)
+            cells = [field_ref[c, x, y, :, spot] for y in range(eyd)]
+            for y in range(eyd):
+                if y + 1 < eyd:
+                    above = pltpu.roll(cells[y + 1], 56, 1)
+                else:
+                    above = pltpu.roll(far_lo, (56 - 8 * q) % 128, 1)
+                if y > 0:
+                    below = pltpu.roll(cells[y - 1], 72, 1)
+                else:
+                    below = pltpu.roll(far_hi, (72 + 8 * q) % 128, 1)
+                v = cells[y] + jnp.where(place >= 56, above, 0.0) + jnp.where(place < 8, below, 0.0)
+                nxt = pltpu.roll(pltpu.roll(v, ez - 1, 0), 7, 1)
+                prv = pltpu.roll(pltpu.roll(v, 1, 0), 121, 1)
+                buf_ref[c, x, y, :, spot] = v + jnp.where(up, nxt, 0.0) + jnp.where(down, prv, 0.0)
+        out_copy(c, x).start()
+        return carry
+
+    lax.fori_loop(0, 3 * exd, layer, 0)
 
     def pick(index, carry):
         held = [ret_ref[position_ref[index * 8 + u]] for u in range(8)]
@@ -483,8 +486,12 @@
         return carry
 
     lax.fori_loop(0, ret_ref.shape[0] // 8, pick, 0)
-    for copy in copies:
-        copy.wait()
+
+    def drain(index, carry):
+        out_copy(lax.div(index, exd), lax.rem(index, exd)).wait()
+        return carry
+
+    lax.fori_loop(0, 3 * exd, drain, 0)
 
 
 def run_yz(position, field, far_lo, far_hi, ret):
@@ -501,9 +508,13 @@
 
 
 def send_kernel(
-    n_gy, sorting_ref, pos_ref, vel_ref, coef_ref, label_ref,
-    got_ref, got_label_ref, send_ref, sem, label_sem,
+    n_gy, sorting_ref, pos_hbm, vel_hbm, coef_hbm, label_ref,
+    got_ref, got_label_ref, pos_ref, vel_ref, coef_ref, send_ref, sem, label_sem, in_sem,
 ):
+    pairs = ((pos_hbm, pos_ref), (vel_hbm, vel_ref), (coef_hbm, coef_ref))
+    inputs = [pltpu.make_async_copy(src, dst, in_sem.at[i]) for i, (src, dst) in enumerate(pairs)]
+    for copy in inputs:
+        copy.start()
     share = pos_ref.shape[1] // n_gy
     gy = lax.axis_index("gy")
     mesh_id = pl.DeviceIdType.MESH
@@ -543,6 +554,8 @@
         lax.fori_loop(0, share // 4, some, 0)
 
     order = sorted(range(1, n_gy), key=lambda off: -min(off, n_gy - off))
+    for copy in inputs:
+        copy.wait()
     for place, off in enumerate(order):
         pack(send_ref, lax.rem(gy + off, n_gy) * share)
         if place == 0:
@@ -569,18 +582,24 @@
             jax.ShapeDtypeStruct((elems, 8, 128), f32),
             jax.ShapeDtypeStruct(label.shape, f32),
         ),
-        in_specs=[pl.BlockSpec(memory_space=SMEM)] + [pl.BlockSpec(memory_space=VMEM)] * 4,
+        in_specs=[pl.BlockSpec(memory_space=SMEM)]
+        + [pl.BlockSpec(memory_space=pltpu.HBM)] * 3
+        + [pl.BlockSpec(memory_space=VMEM)],
         out_specs=[pl.BlockSpec(memory_space=VMEM)] * 2,
         scratch_shapes=[
+            pltpu.VMEM(pos.shape, f32),
+            pltpu.VMEM(vel.shape, f32),
+            pltpu.VMEM(coef.shape, f32),
             pltpu.VMEM((elems, 8, 128), f32),
             dma((2, n_gy - 1)),
             dma((2, n_gy - 1)),
+            dma((3,)),
         ],
         compiler_params=pltpu.CompilerParams(
             vmem_limit_bytes=32 * 1024 * 1024, collective_id=1, has_side_effects=True
         ),
         name="migrate",
-    )(sorting, pos, vel, coef, label)
+    )(sorting, *(pltpu.with_memory_space_constraint(x, pltpu.HBM) for x in (pos, vel, coef)), label)
 
 
 def inverse_of(position):

time: 49.2 us -> 42.2 us (0.86)
  Pallas kernels: 43.8 us -> 39.2 us
  local copies, waits for them, and re-layouts: 3.98 us -> 0.09 us
  other arithmetic: 0.59 us -> 2.01 us
    pallas_call x1, Pallas kernels: 8.17 us -> 3.61 us  [run_yz(): pl.pallas_call(yz_pass, out_shape=(jax.ShapeDtypeStruct(field.shape, f32)...]
    unnamed x14 -> x2, local copies, waits for them, and re-layouts: 3.9 us -> 0.01 us
    reduce_sum x1, other arithmetic: 0.17 us -> 0.9 us  [body(): position = dest * share + jnp.sum(earlier.astype(jnp.int32), axis=1)]
    add x1, other arithmetic: 0.01 us -> 0.71 us  [body(): room = position // share * lanes + position % share]
where the time goes in v1:
time: 42.2 us; the launch traced here: 42 us
  Pallas kernels  39.2 us (93%)
  other arithmetic  2.01 us (5%)
  between operations  0.68 us (2%)
    pallas_call x1, Pallas kernels, run_main(): pl.pallas_call(functools.partial(main_kernel, shape, chunks, n_gx, n_gy),...  25.9 us
    pallas_call x1, Pallas kernels, run_send(): pl.pallas_call(functools.partial(send_kernel, n_gy), out_shape=(jax.Shape...  9.74 us
    pallas_call x1, Pallas kernels, run_yz(): pl.pallas_call(yz_pass, out_shape=(jax.ShapeDtypeStruct(field.shape, f32)...  3.61 us
    reduce_sum x1, other arithmetic, body(): position = dest * share + jnp.sum(earlier.astype(jnp.int32), axis=1)  0.9 us

profile of v1, /device:TPU:9, one launch (start us, length us, event | category | flops | bytes accessed | tf_op | source)
XLA Modules:
  0.0 42.0 jit_solution(4988401443542786698)
XLA Ops:
  0.6 0.0 copy-start
  0.6 0.9 %convert_reduce_fusion = s32[128]{0:T(128)S(1)} fusion(s32[128]{0:T(128)} %param.12), kind=kLoop, calls=%fused_computation.6 | loop fusion | flops 81792 | bytes 1024 | tf_op jit(solution)/shard_map/reduce_sum | solution.py:619
  1.5 0.7 %fusion.1 = (s32[128]{0:T(128)S(1)}, s32[128]{0:T(128)S(1)}, s32[128]{0:T(128)S(1)}) fusion(s32[128]{0:T(128)S(1)} %convert_reduce_fusion, s32[128]{0:T(128)} %param.12, s32[128]{0:T(128)} %param.11, s32[128]{0:T(128)} %param.13), kind=kLoop, calls=%fused_computation.20 | loop fusion | flops 3200 | bytes 3584 | tf_op jit(solution)/shard_map/add | solution.py:623
  2.3 0.1 select_reduce_fusion.2.sorting_ref
  2.4 0.2 select_reduce_fusion
  2.5 9.7 %migrate.1 = (f32[128,8,128]{2,1,0:T(8,128)S(1)}, f32[4,1,128]{2,1,0:T(1,128)S(1)}) custom-call(s32[128]{0:T(128)S(1)} %select_reduce_fusion.2.sorting_ref, f32[3,128,128]{2,1,0:T(8,128)} %bitcast.7, f32[3,128,128]{2,1,0:T(8,128)} %bitcast.8, f32[128,2,128]{2,1,0:T(2,128)} %coef_hbm.1, f32[4,1,128]{2,1,0:T(1,128)S(1)} %bitcast.5), custom_call_target="tpu_custom_call" | custom-call | tf_op jit(solution)/shard_map/migrate/pallas_call | solution.py:579
  12.3 0.1 convert_element_type.30
  12.4 0.1 select_reduce_fusion.1.slot_ref
  12.5 0.0 copy-done
  12.5 25.9 %elements.1 = (f32[3,2,4,16,512]{4,3,2,1,0:T(8,128)S(1)}, f32[3,2,16,128]{3,2,1,0:T(8,128)S(1)}, f32[3,2,16,128]{3,2,1,0:T(8,128)S(1)}, f32[128,3,128]{2,1,0:T(4,128)S(1)}) custom-call(s32[128]{0:T(128)S(1)} %select_reduce_fusion.1.slot_ref, s32[128]{0:T(128)S(1)} %get-tuple-element.20.count_ref, s32[128]{0:T(128)S(1)} %get-tuple-element.21.elem_ref, ...), custom_call_target="tpu_custom_call" | custom-call | flops 200000000 | bytes 4000000 | tf_op jit(solution)/shard_map/elements/pallas_call | solution.py:405
  38.4 3.6 %yzpass.1 = (f32[3,2,4,16,512]{4,3,2,1,0:T(8,128)}, f32[3,128,128]{2,1,0:T(8,128)}) custom-call(s32[128]{0:T(128)S(1)} %get-tuple-element.19.position_ref, f32[3,2,4,16,512]{4,3,2,1,0:T(8,128)S(1)} %get-tuple-element.12.field_ref, f32[3,2,16,128]{3,2,1,0:T(8,128)S(1)} %get-tuple-element.13.far_lo_ref, f32[3,2,16,128]{3,2,1,0:T(8,128)S(1)} %get-tuple-element.14.far_hi_ref, ...), custom_call_target="tpu_custom_call" | custom-call | tf_op jit(solution)/shard_map/yzpass/pallas_call | solution.py:499
  (3 shorter events, 0.0 us)
Async XLA Ops:
  0.6 11.9 %copy-start = (bf16[3,2,4,16,512]{4,3,2,1,0:T(8,128)(2,1)S(1)}, bf16[3,2,4,16,512]{4,3,2,1,0:T(8,128)(2,1)}, u32[]{:S(2)}) copy-start(bf16[3,2,4,16,512]{4,3,2,1,0:T(8,128)(2,1)} %param.7) | copy-start | bytes 1179652

commit v2 on v1

v2 whole, which is shorter than its diff:
```python
import functools
import math

import jax
import jax.numpy as jnp
from jax import lax
from jax.experimental import pallas as pl
from jax.experimental.pallas import tpu as pltpu
from jax.sharding import PartitionSpec as P

GLL = (
    -1.0,
    -0.8717401485096066,
    -0.5917001814331423,
    -0.2092992179024789,
    0.2092992179024789,
    0.5917001814331423,
    0.8717401485096066,
    1.0,
)
SHARPNESS = 8.0
WIDTH = math.sqrt(SHARPNESS * math.log2(math.e))
VMEM = pltpu.VMEM
SMEM = pltpu.SMEM
ROWS = 24


def lane_iota(shape):
    return lax.broadcasted_iota(jnp.int32, shape, len(shape) - 1)


def node_consts():
    row = lax.broadcasted_iota(jnp.int32, (8, 128), 0)

    def pick(values):
        out = jnp.full((8, 128), values[7], jnp.float32)
        for i in range(7):
            out = jnp.where(row == i, jnp.float32(values[i]), out)
        return out

    others = [pick([[GLL[m] for m in range(8) if m != i][n] for i in range(8)]) for n in range(7)]
    scales = []
    for i in range(8):
        product = 1.0
        for m in range(8):
            if m != i:
                product *= GLL[i] - GLL[m]
        scales.append(1.0 / product)
    return pick(GLL), others, pick(scales)


def lagrange(x, others, scale):
    diffs = [x - o for o in others]
    left = (diffs[0] * diffs[1]) * (diffs[2] * diffs[3])
    right = (diffs[4] * diffs[5]) * (diffs[6] * scale)
    return left * right


def gauss(x, nodes):
    gap = nodes - x
    return jnp.exp2(-(gap * gap))


def split(x):
    high = x.astype(jnp.bfloat16)
    low = (x - high.astype(jnp.float32)).astype(jnp.bfloat16)
    return high, low


def planes(a, b):
    return jnp.concatenate([a[j : j + 1] * b for j in range(8)], axis=0)


def spread_nodes(vel_ref, vs_ref, elems):
    low = lane_iota((elems, 128)) < 64
    for c in range(3):
        for q in range(4):
            x = vel_ref[c, :, q * 128 : (q + 1) * 128].astype(jnp.float32)
            turned = pltpu.roll(x, 64, 1)
            vs_ref[pl.ds(c * 8 + 2 * q, elems, stride=ROWS), :] = jnp.where(low, x, turned)
            vs_ref[pl.ds(c * 8 + 2 * q + 1, elems, stride=ROWS), :] = jnp.where(low, turned, x)


def rows_of(refs):
    return jnp.concatenate(refs, axis=0)


def project(left, high, low):
    top, rest = split(left)
    both = jnp.concatenate([jnp.concatenate([top, top], axis=1), jnp.concatenate([rest, rest], axis=1)], axis=0)
    out = lax.dot_general(
        both, jnp.concatenate([high, low], axis=1), (((1,), (1,)), ((), ())), preferred_element_type=jnp.float32
    )
    return out[: left.shape[0]] + out[left.shape[0] :]


def st_planes(s, t, nodes):
    return split(planes(gauss(s, nodes), gauss(t, nodes)))


def line(ref, c, at):
    return ref[c, pl.ds(at, 1), :]


def wide_line(ref, c, at):
    return jnp.broadcast_to(line(ref, c, at), (8, 128))


def main_kernel(
    shape, n_gx, n_gy,
    sorting_ref, count_ref, label_ref, pos_hbm, vel_hbm, coef_hbm, velocity_hbm,
    field_ref, far_lo_ref, far_hi_ref, ret_ref,
    pos_in, vel_in, coef_in, vel_ref, send_pos, send_rest, got_pos, got_rest, got_label, slot_row, tag_s, slot_s,
    vs_ref, fluid_ref, drag_ref, dep_ref, ts_ref, fs_ref,
    pos_ref, gpos_ref, out_ref, gdrag_ref, face_ref, gface_ref, lo_ref, hi_ref,
    in_sem, label_sem, block_sem, rest_sem, tag_sem, pos_sem, drag_sem, face_sem, y_sem, back_sem,
):
    exd, eyd, ez = shape
    elems = exd * eyd * ez
    columns = eyd * ez
    share = elems // n_gy
    half = columns // 2
    group = 16
    per = share // group
    near = n_gy // 2
    i32 = jnp.int32
    gx = lax.axis_index("gx")
    gy = lax.axis_index("gy")
    has = (gx > 0, gx < n_gx - 1)
    mesh_id = pl.DeviceIdType.MESH

    def partner(m):
        total, bit = 0, 1
        while bit < n_gy:
            total = total + lax.rem(lax.div(gy, bit) + lax.div(m, bit), 2) * bit
            bit *= 2
        return total

    pairs = ((pos_hbm, pos_in), (vel_hbm, vel_in), (coef_hbm, coef_in), (velocity_hbm, vel_ref))
    inputs = [pltpu.make_async_copy(src, dst, in_sem.at[i]) for i, (src, dst) in enumerate(pairs)]
    for copy in inputs:
        copy.start()

    def side_id(side):
        return {"gx": gx - 1 if side == 0 else gx + 1}

    def to_side(side, src, dst, sems, *at):
        return pltpu.make_async_remote_copy(
            src_ref=src, dst_ref=dst, send_sem=sems.at[(0, side) + at], recv_sem=sems.at[(1, 1 - side) + at],
            device_id=side_id(side), device_id_type=mesh_id,
        )

    def from_side(side, src, dst, sems, *at):
        return pltpu.make_async_remote_copy(
            src_ref=src, dst_ref=dst, send_sem=sems.at[(0, side) + at], recv_sem=sems.at[(1, side) + at],
            device_id=side_id(side), device_id_type=mesh_id,
        )

    barrier = pltpu.get_barrier_semaphore()
    for side in range(2):
        @pl.when(has[side])
        def _():
            pl.semaphore_signal(barrier, inc=1, device_id=side_id(side), device_id_type=mesh_id)
    for m in range(1, n_gy):
        pl.semaphore_signal(barrier, inc=1, device_id={"gy": partner(m)}, device_id_type=mesh_id)

    def peer_copy(src, dst, sems, m):
        return pltpu.make_async_remote_copy(
            src_ref=src, dst_ref=dst, send_sem=sems.at[0, m - 1], recv_sem=sems.at[1, m - 1],
            device_id={"gy": partner(m)}, device_id_type=mesh_id,
        )

    def part(index):
        return pl.ds(pl.multiple_of(index * share, 8), share)

    def label_copy(m):
        return peer_copy(label_ref.at[partner(m)], got_label.at[gy], label_sem, m)

    def pos_copy(m):
        return peer_copy(send_pos.at[:, part(partner(m))], got_pos.at[:, part(gy)], block_sem, m)

    def rest_copy(m):
        return peer_copy(send_rest.at[:, part(partner(m))], got_rest.at[:, part(gy)], rest_sem, m)

    def back_copy(m):
        return peer_copy(drag_ref.at[:, part(partner(m))], ret_ref.at[:, part(gy)], back_sem, m)

    def tag_copy(index, m):
        return pltpu.make_async_copy(got_label.at[index], tag_s.at[index], tag_sem.at[m])

    lane = lane_iota((1, 128))

    def pack_pos(dst, index):
        def some(i, carry):
            start = pl.multiple_of(index * share + i * 8, 8)
            spots = [sorting_ref[start + u] for u in range(8)]
            for c in range(3):
                dst[c, pl.ds(start, 8), :] = rows_of([line(pos_in, c, b) for b in spots])
            return carry

        lax.fori_loop(0, share // 8, some, 0)

    def pack_rest(dst, index):
        def some(i, carry):
            start = pl.multiple_of(index * share + i * 8, 8)
            spots = [sorting_ref[start + u] for u in range(8)]
            for c in range(3):
                dst[c, pl.ds(start, 8), :] = rows_of([line(vel_in, c, b) for b in spots])
            dst[3, pl.ds(start, 8), :] = rows_of(
                [jnp.where(lane < count_ref[b], coef_in[b, 0:1, :], 0.0) for b in spots]
            )
            dst[4, pl.ds(start, 8), :] = rows_of([coef_in[b, 1:2, :] for b in spots])
            return carry

        lax.fori_loop(0, share // 8, some, 0)

    got_label[gy] = label_ref[gy]
    tag_copy(gy, 0).start()
    order = tuple(range(near, n_gy)) + tuple(range(1, near))
    inputs[0].wait()
    for m in order[: n_gy - near]:
        pack_pos(send_pos, partner(m))
    pl.semaphore_wait(barrier, n_gy - 1 + has[0].astype(i32) + has[1].astype(i32))
    for m in order:
        label_copy(m).start()
    for m in order[: n_gy - near]:
        pos_copy(m).start()
    inputs[1].wait()
    inputs[2].wait()
    for m in order[: n_gy - near]:
        pack_rest(send_rest, partner(m))
        rest_copy(m).start()
    for m in order[n_gy - near :]:
        pack_pos(send_pos, partner(m))
        pos_copy(m).start()
        pack_rest(send_rest, partner(m))
        rest_copy(m).start()
    pack_pos(got_pos, gy)
    pack_rest(got_rest, gy)
    inputs[3].wait()
    spread_nodes(vel_ref, vs_ref, elems)
    consts = node_consts()
    nodes, others, scale = consts
    nodes = nodes * WIDTH
    tag_copy(gy, 0).wait()

    def slot_of(e):
        return slot_s[0, e]

    def collect(dst, src, start, count):
        def some(i, carry):
            for side in range(2):
                at = pl.multiple_of(start + i * 8, 8)
                spots = [slot_of(side * columns + at + u) for u in range(8)]
                for c in range(3):
                    dst[side, c, pl.ds(at, 8), :] = rows_of([line(src, c, b) for b in spots])
            return carry

        lax.fori_loop(0, count // 8, some, 0)

    def interpolate(index, carry):
        for m in range(1, near):
            @pl.when(index == m * per)
            def _():
                label_copy(m).wait()
                tag_copy(partner(m), m).start()
                pos_copy(m).wait()
                tag_copy(partner(m), m).wait()

        @pl.when(index == near * per)
        def _():
            for m in range(near, n_gy):
                label_copy(m).wait()
                tag_copy(partner(m), m).start()
            total = got_label[0]
            for other in range(1, n_gy):
                total = total + got_label[other]
            slot_row[...] = total[:, 128:]
            copy = pltpu.make_async_copy(slot_row, slot_s, tag_sem.at[n_gy])
            copy.start()
            for m in range(near, n_gy):
                tag_copy(partner(m), m).wait()
            copy.wait()
            for m in range(near, n_gy):
                pos_copy(m).wait()
            collect(pos_ref, got_pos, 0, columns)
            for side in range(2):
                @pl.when(has[side])
                def _():
                    to_side(side, pos_ref.at[side], gpos_ref.at[1 - side], pos_sem).start()

        source = partner(lax.div(index, per))
        first = lax.rem(index, per) * group
        for batch in range(group // 8):
            fluid = [[], [], []]
            for u in range(8):
                i = first + batch * 8 + u
                slot = source * share + i
                e = tag_s[source, 0, i]
                r, s, t = (wide_line(got_pos, d, slot) for d in range(3))
                basis_r = lagrange(r, others, scale)
                high, low = split(planes(lagrange(s, others, scale), lagrange(t, others, scale)))
                partial = jnp.dot(
                    vs_ref[pl.ds(e * ROWS, ROWS), :].astype(jnp.bfloat16),
                    jnp.concatenate([high, low], axis=0),
                    preferred_element_type=jnp.float32,
                )
                for c in range(3):
                    fluid[c].append(jnp.sum(partial[c * 8 : c * 8 + 8] * basis_r, axis=0, keepdims=True))
            at = pl.multiple_of(source * share + first + batch * 8, 8)
            for c in range(3):
                fluid_ref[c, pl.ds(at, 8), :] = rows_of(fluid[c])
        return carry

    lax.fori_loop(0, elems // group, interpolate, 0)

    def forces(start, count):
        def some(i, carry):
            m = lax.div(start + i * 8, share)
            at = pl.ds(pl.multiple_of(partner(m) * share + lax.rem(start + i * 8, share), 8), 8)
            rel = [fluid_ref[c, at, :] - got_rest[c, at, :] for c in range(3)]
            speed = jnp.sqrt(rel[0] * rel[0] + rel[1] * rel[1] + rel[2] * rel[2])
            power = jnp.exp(0.687 * jnp.log(got_rest[4, at, :] * speed))
            factor = got_rest[3, at, :] * (1.0 + 0.15 * power)
            for c in range(3):
                drag_ref[c, at, :] = factor * rel[c]
            return carry

        lax.fori_loop(0, count // 8, some, 0)

    def strip(k):
        return lax.rem(k * (eyd - 1), eyd)

    def drag_copy(make, side, y):
        at = pl.ds(pl.multiple_of(y * ez, 8), ez)
        return make(side, out_ref.at[side, :, at], gdrag_ref.at[1 - side, :, at], drag_sem, y)

    def deposit(index, carry):
        @pl.when(index == 0)
        def _():
            for m in range(1, near):
                rest_copy(m).wait()
            forces(0, near * share)

        @pl.when(index == near * per)
        def _():
            for m in range(near, n_gy):
                rest_copy(m).wait()
            forces(near * share, elems - near * share)
            for k in range(eyd):
                y = k * (eyd - 1) % eyd
                collect(out_ref, drag_ref, y * ez, ez)
                for side in range(2):
                    @pl.when(has[side])
                    def _():
                        drag_copy(to_side, side, y).start()
            for m in order:
                back_copy(m).start()
            ret_ref[:, part(gy), :] = drag_ref[:, part(gy), :]

        source = partner(lax.div(index, per))
        first = lax.rem(index, per) * group
        for u in range(group):
            i = first + u
            slot = source * share + i
            layer = jnp.full((8, 128), tag_s[source, 0, i], i32)
            shift = jnp.where(layer < columns, -2.0 * WIDTH, 2.0 * WIDTH)
            r, s, t = (wide_line(got_pos, d, slot) * WIDTH for d in range(3))
            weights = (gauss(r, nodes), gauss(r + shift, nodes))
            force = [-line(drag_ref, c, slot) for c in range(3)]
            left = jnp.concatenate([f * w for w in weights for f in force], axis=0)
            out = project(left, *st_planes(s, t, nodes))
            dep_ref[pl.ds(pl.multiple_of(slot * 2 * ROWS, 8), 2 * ROWS), 0:64] = out
        return carry

    lax.fori_loop(0, elems // group, deposit, 0)

    def gather(i, carry):
        for side in range(exd):
            spots = []
            for u in range(8):
                col = i * 8 + u
                mine = slot_of(side * columns + col) * (2 * ROWS)
                other = slot_of((1 - side) * columns + col) * (2 * ROWS) + ROWS
                e = side * columns + col
                ts_ref[pl.ds(pl.multiple_of(e * ROWS, 8), ROWS), :] = (
                    dep_ref[pl.ds(mine, ROWS), :] + dep_ref[pl.ds(other, ROWS), :]
                )
                spots.append(mine)
            node = 0 if side == 0 else 7
            for c in range(3):
                fs_ref[side, c, pl.ds(pl.multiple_of(i * 8, 8), 8), :] = rows_of(
                    [dep_ref[pl.ds(at + c * 8 + node, 1), :] for at in spots]
                )
        return carry

    lax.fori_loop(0, columns // 8, gather, 0)

    base = (0, elems - columns)
    low_h = lane_iota((half, 128)) < 64
    for side in range(2):
        node = 0 if side == 0 else 7
        for c in range(3):
            one = ts_ref[pl.ds(base[side] * ROWS + c * 8 + node, half, stride=ROWS), :]
            two = ts_ref[pl.ds((base[side] + half) * ROWS + c * 8 + node, half, stride=ROWS), :]
            face_ref[side, c] = jnp.where(low_h, one, pltpu.roll(two, 64, 1))
        @pl.when(has[side])
        def _():
            to_side(side, face_ref.at[side], gface_ref.at[1 - side], face_sem).start()

    for side in range(2):
        @pl.when(has[side])
        def _():
            from_side(side, pos_ref.at[side], gpos_ref.at[side], pos_sem).wait()

    def ghost(k, carry):
        y = strip(k)
        for side in range(2):
            @pl.when(has[side])
            def _():
                at = pl.ds(pl.multiple_of(y * ez, 8), ez)
                from_side(side, out_ref.at[side, :, at], gdrag_ref.at[side, :, at], drag_sem, y).wait()
                sums = []
                for g in range(ez):
                    col = y * ez + g
                    r, s, t = (jnp.broadcast_to(gpos_ref[side, d, pl.ds(col, 1), :], (8, 128)) * WIDTH for d in range(3))
                    weight = gauss(r + (-2.0 if side == 0 else 2.0) * WIDTH, nodes)
                    left = jnp.concatenate([(-gdrag_ref[side, c, pl.ds(col, 1), :]) * weight for c in range(3)], axis=0)
                    add = project(left, *st_planes(s, t, nodes))
                    spot = pl.ds(pl.multiple_of((base[side] + col) * ROWS, 8), ROWS)
                    sums.append((spot, ts_ref[spot, 0:64] + add))
                for spot, value in sums:
                    ts_ref[spot, 0:64] = value
        return carry

    lax.fori_loop(0, eyd, ghost, 0)

    for side in range(2):
        @pl.when(has[side])
        def _():
            from_side(side, face_ref.at[side], gface_ref.at[side], face_sem).wait()

    low = lane_iota((ez, 128)) < 64
    spot64 = lane_iota((ez, 128)) % 64
    lo_copy = pltpu.make_async_remote_copy(
        src_ref=lo_ref, dst_ref=far_lo_ref, send_sem=y_sem.at[0, 0], recv_sem=y_sem.at[1, 0],
        device_id={"gy": gy - 1}, device_id_type=mesh_id,
    )
    hi_copy = pltpu.make_async_remote_copy(
        src_ref=hi_ref, dst_ref=far_hi_ref, send_sem=y_sem.at[0, 1], recv_sem=y_sem.at[1, 1],
        device_id={"gy": gy + 1}, device_id_type=mesh_id,
    )

    def assemble(index, carry):
        k, c = lax.div(index, 3), lax.rem(index, 3)
        y = strip(k)
        upper = y >= eyd // 2

        def lanes(x, q):
            start = (x * columns + y * ez) * ROWS + c * 8 + 2 * q
            even = ts_ref[pl.ds(start, ez, stride=ROWS), :]
            odd = ts_ref[pl.ds(start + 1, ez, stride=ROWS), :]
            return jnp.where(low, even, pltpu.roll(odd, 64, 1))

        def far(side):
            came = gface_ref[side, c, pl.ds(pl.multiple_of(lax.rem(y, eyd // 2) * ez, 8), ez), :]
            turned = pltpu.roll(came, 64, 1)
            came = jnp.where(low != upper, came, turned)
            mine = fs_ref[side, c, pl.ds(pl.multiple_of(y * ez, 8), ez), :]
            mine = jnp.where(low, mine, pltpu.roll(mine, 64, 1))
            return jnp.where(has[side], came + mine, 0.0)

        grid = [[lanes(x, q) for q in range(4)] for x in range(exd)]
        for x in range(exd):
            above = pltpu.roll(grid[x + 1][0], 64, 1) if x + 1 < exd else far(1)
            below = pltpu.roll(grid[x - 1][3], 64, 1) if x > 0 else far(0)
            done = list(grid[x])
            done[3] = done[3] + jnp.where(low, 0.0, above)
            done[0] = done[0] + jnp.where(low, below, 0.0)
            for q in range(4):
                field_ref[c, x, y, :, q * 128 : (q + 1) * 128] = done[q]

            @pl.when(k == 0)
            def _():
                face = jnp.where(spot64 < 8, done[0], 0.0)
                for q in range(1, 4):
                    face = face + pltpu.roll(jnp.where(spot64 < 8, done[q], 0.0), 8 * q, 1)
                lo_ref[c, x] = face

            @pl.when(k == 1)
            def _():
                face = jnp.where(spot64 >= 56, done[0], 0.0)
                for q in range(1, 4):
                    face = face + pltpu.roll(jnp.where(spot64 >= 56, done[q], 0.0), 128 - 8 * q, 1)
                hi_ref[c, x] = face

        @pl.when((index == 2) & (gy > 0))
        def _():
            lo_copy.start()

        @pl.when((index == 5) & (gy < n_gy - 1))
        def _():
            hi_copy.start()

        return carry

    lax.fori_loop(0, 3 * eyd, assemble, 0)

    @pl.when(gy > 0)
    def _():
        lo_copy.wait_send()
        hi_copy.wait_recv()

    @pl.when(gy < n_gy - 1)
    def _():
        hi_copy.wait_send()
        lo_copy.wait_recv()

    for m in order:
        back_copy(m).wait()


def run_main(sorting, counts, label, pos, vel, coef, velocity, shape):
    exd, eyd, ez = shape
    elems = exd * eyd * ez
    columns = eyd * ez
    n_gx, n_gy = lax.axis_size("gx"), lax.axis_size("gy")
    f32, i32 = jnp.float32, jnp.int32
    dma = pltpu.SemaphoreType.DMA
    face = (3, exd, ez, 128)
    strips = (2, 3, columns, 128)
    hbm = [pltpu.with_memory_space_constraint(x, pltpu.HBM) for x in (pos, vel, coef, velocity)]
    return pl.pallas_call(
        functools.partial(main_kernel, shape, n_gx, n_gy),
        out_shape=(
            jax.ShapeDtypeStruct((3, exd, eyd, ez, 512), f32),
            jax.ShapeDtypeStruct(face, f32),
            jax.ShapeDtypeStruct(face, f32),
            jax.ShapeDtypeStruct((3, elems, 128), f32),
        ),
        in_specs=[pl.BlockSpec(memory_space=SMEM)] * 2
        + [pl.BlockSpec(memory_space=VMEM)]
        + [pl.BlockSpec(memory_space=pltpu.HBM)] * 4,
        out_specs=[pl.BlockSpec(memory_space=VMEM)] * 4,
        scratch_shapes=[
            pltpu.VMEM(pos.shape, f32),
            pltpu.VMEM(vel.shape, f32),
            pltpu.VMEM(coef.shape, f32),
            pltpu.VMEM(velocity.shape, velocity.dtype),
            pltpu.VMEM((3, elems, 128), f32),
            pltpu.VMEM((5, elems, 128), f32),
            pltpu.VMEM((3, elems, 128), f32),
            pltpu.VMEM((5, elems, 128), f32),
            pltpu.VMEM(label.shape, i32),
            pltpu.VMEM((1, 128), i32),
            pltpu.SMEM(label.shape, i32),
            pltpu.SMEM((1, 128), i32),
            pltpu.VMEM((elems * ROWS, 128), f32),
            pltpu.VMEM((3, elems, 128), f32),
            pltpu.VMEM((3, elems, 128), f32),
            pltpu.VMEM((elems * 2 * ROWS, 128), f32),
            pltpu.VMEM((elems * ROWS, 128), f32),
            pltpu.VMEM(strips, f32),
            pltpu.VMEM(strips, f32),
            pltpu.VMEM(strips, f32),
            pltpu.VMEM(strips, f32),
            pltpu.VMEM(strips, f32),
            pltpu.VMEM((2, 3, columns // 2, 128), f32),
            pltpu.VMEM((2, 3, columns // 2, 128), f32),
            pltpu.VMEM(face, f32),
            pltpu.VMEM(face, f32),
            dma((4,)),
            dma((2, n_gy - 1)),
            dma((2, n_gy - 1)),
            dma((2, n_gy - 1)),
            dma((n_gy + 1,)),
            dma((2, 2)),
            dma((2, 2, eyd)),
            dma((2, 2)),
            dma((2, 2)),
            dma((2, n_gy - 1)),
        ],
        compiler_params=pltpu.CompilerParams(
            vmem_limit_bytes=40 * 1024 * 1024, collective_id=0, has_side_effects=True
        ),
        name="elements",
    )(sorting, counts, label, *hbm)


def yz_pass(position_ref, field_ref, far_lo_ref, far_hi_ref, ret_ref, out_ref, drag_ref, buf_ref, sem):
    _, exd, eyd, ez, _ = field_ref.shape
    at = lax.axis_index("gy")
    first = at > 0
    last = at < lax.axis_size("gy") - 1
    place = lane_iota((ez, 128)) % 64
    k = lane_iota((ez, 128)) % 8
    row = lax.broadcasted_iota(jnp.int32, (ez, 128), 0)
    up = (k == 7) & (row < ez - 1)
    down = (k == 0) & (row > 0)

    def out_copy(c, x):
        return pltpu.make_async_copy(buf_ref.at[c, x], out_ref.at[c, x], sem.at[c, x])

    def layer(index, carry):
        c, x = lax.div(index, exd), lax.rem(index, exd)
        far_lo = jnp.where(last, far_lo_ref[c, x], 0.0)
        far_hi = jnp.where(first, far_hi_ref[c, x], 0.0)
        for q in range(4):
            spot = slice(q * 128, (q + 1) * 128)
            cells = [field_ref[c, x, y, :, spot] for y in range(eyd)]
            for y in range(eyd):
                if y + 1 < eyd:
                    above = pltpu.roll(cells[y + 1], 56, 1)
                else:
                    above = pltpu.roll(far_lo, (56 - 8 * q) % 128, 1)
                if y > 0:
                    below = pltpu.roll(cells[y - 1], 72, 1)
                else:
                    below = pltpu.roll(far_hi, (72 + 8 * q) % 128, 1)
                v = cells[y] + jnp.where(place >= 56, above, 0.0) + jnp.where(place < 8, below, 0.0)
                nxt = pltpu.roll(pltpu.roll(v, ez - 1, 0), 7, 1)
                prv = pltpu.roll(pltpu.roll(v, 1, 0), 121, 1)
                buf_ref[c, x, y, :, spot] = v + jnp.where(up, nxt, 0.0) + jnp.where(down, prv, 0.0)
        out_copy(c, x).start()
        return carry

    lax.fori_loop(0, 3 * exd, layer, 0)

    def pick(index, carry):
        spots = [position_ref[index * 8 + u] for u in range(8)]
        for c in range(3):
            drag_ref[c, pl.ds(pl.multiple_of(index * 8, 8), 8), :] = rows_of([line(ret_ref, c, at) for at in spots])
        return carry

    lax.fori_loop(0, ret_ref.shape[1] // 8, pick, 0)

    def drain(index, carry):
        out_copy(lax.div(index, exd), lax.rem(index, exd)).wait()
        return carry

    lax.fori_loop(0, 3 * exd, drain, 0)


def run_yz(position, field, far_lo, far_hi, ret):
    f32 = jnp.float32
    return pl.pallas_call(
        yz_pass,
        out_shape=(jax.ShapeDtypeStruct(field.shape, f32), jax.ShapeDtypeStruct(ret.shape, f32)),
        in_specs=[pl.BlockSpec(memory_space=SMEM)] + [pl.BlockSpec(memory_space=VMEM)] * 4,
        out_specs=[pl.BlockSpec(memory_space=pl.ANY), pl.BlockSpec(memory_space=VMEM)],
        scratch_shapes=[pltpu.VMEM(field.shape, f32), pltpu.SemaphoreType.DMA(field.shape[:2])],
        compiler_params=pltpu.CompilerParams(vmem_limit_bytes=32 * 1024 * 1024),
        name="yzpass",
    )(position, field, far_lo, far_hi, ret)


def inverse_of(position):
    n = position.shape[0]
    ladder = jnp.arange(n, dtype=jnp.int32)
    return jnp.sum(jnp.where(position[None, :] == ladder[:, None], ladder[None, :], 0), axis=1)


def body(velocity, part_pos, part_vel, part_coef, counts, dest, elem):
    _, exd, eyd, ez, nodes = velocity.shape
    elems = exd * eyd * ez
    devices = lax.axis_size("gy")
    share = elems // devices
    ladder = jnp.arange(elems, dtype=jnp.int32)
    earlier = (dest[None, :] == dest[:, None]) & (ladder[None, :] < ladder[:, None])
    rank = jnp.sum(earlier.astype(jnp.int32), axis=1)
    position = dest * share + rank
    sorting = inverse_of(position)
    cells = jnp.arange(devices * 256, dtype=jnp.int32)[:, None]
    tags = jnp.where(cells == (dest * 256 + rank)[None, :], elem[None, :], 0)
    slots = jnp.where(
        cells == (dest * 256 + 128 + elem)[None, :], (lax.axis_index("gy") * share + rank)[None, :], 0
    )
    label = jnp.sum(tags + slots, axis=1).reshape(devices, 1, 256)
    field, far_lo, far_hi, ret = run_main(
        sorting, counts, label, part_pos.transpose(1, 0, 2), part_vel.transpose(1, 0, 2), part_coef,
        velocity.reshape(3, elems, nodes), (exd, eyd, ez),
    )
    source, drag_out = run_yz(position, field, far_lo, far_hi, ret)
    return (drag_out.transpose(1, 0, 2), source)


def solution(mesh):
    in_specs = (
        P(None, "gx", "gy", None, None),
        P(("gx", "gy"), None, None),
        P(("gx", "gy"), None, None),
        P(("gx", "gy"), None, None),
        P(("gx", "gy")),
        P(("gx", "gy")),
        P(("gx", "gy")),
    )
    out_specs = (P(("gx", "gy"), None, None), P(None, "gx", "gy", None, None))
    return jax.shard_map(body, mesh=mesh, in_specs=in_specs, out_specs=out_specs, check_vma=False)
```

time: 42.2 us -> 31.4 us (0.74)
  Pallas kernels: 39.2 us -> 27.9 us
  local copies, waits for them, and re-layouts: 0.09 us -> 1.78 us
  other arithmetic: 2.01 us -> 0.5 us
    pallas_call x2 -> x1, Pallas kernels: 35.6 us -> 24.3 us  [run_main(): pl.pallas_call(functools.partial(main_kernel, shape, n_gx, n_gy), out_sha...]
    unnamed x2 -> x6, local copies, waits for them, and re-layouts: 0.01 us -> 1.78 us
    add x1, other arithmetic: 0.71 us -> 0.01 us  [body(): tags = jnp.where(cells == (dest * 256 + rank)[None, :], elem[None, :], 0)]
    reduce_sum x2, other arithmetic: 1.06 us -> 0.39 us  [the longest x1 0.22 us: body(): label = jnp.sum(tags + slots, axis=1).reshape(devices, 1, 256)]
where the time goes in v2:
time: 31.4 us; the launch traced here: 30.8 us
  Pallas kernels  27.9 us (89%)
  local copies, waits for them, and re-layouts  1.78 us (6%)
  between operations  0.67 us (2%)
  other arithmetic  0.5 us (2%)
    pallas_call x1, Pallas kernels, run_main(): pl.pallas_call(functools.partial(main_kernel, shape, n_gx, n_gy), out_sha...  24.3 us
    pallas_call x1, Pallas kernels, run_yz(): pl.pallas_call(yz_pass, out_shape=(jax.ShapeDtypeStruct(field.shape, f32)...  3.61 us
    unnamed x6, local copies, waits for them, and re-layouts  1.78 us

profile of v2, /device:TPU:9, one launch (start us, length us, event | category | flops | bytes accessed | tf_op | source)
XLA Modules:
  0.0 30.8 jit_solution(6124988786672041972)
XLA Ops:
  0.6 0.0 copy-start.2
  0.6 0.6 %copy-done.2 = s32[128]{0:T(128)S(1)} copy-done((s32[128]{0:T(128)S(1)}, s32[128]{0:T(128)}, u32[]{:S(2)}) %copy-start.2) | copy-done | bytes 536
  1.3 0.0 copy-start.1
  1.3 0.2 convert_reduce_fusion
  1.5 0.5 %copy-done.1 = s32[128]{0:T(128)S(1)} copy-done((s32[128]{0:T(128)S(1)}, s32[128]{0:T(128)}, u32[]{:S(2)}) %copy-start.1) | copy-done | bytes 536
  2.0 0.1 select_reduce_fusion.sorting_ref
  2.1 0.2 add_reduce_fusion
  2.3 0.0 copy-start
  2.3 0.6 %copy-done = s32[128]{0:T(128)S(1)} copy-done((s32[128]{0:T(128)S(1)}, s32[128]{0:T(128)}, u32[]{:S(2)}) %copy-start) | copy-done | bytes 536
  2.9 24.3 %elements.1 = (f32[3,2,4,16,512]{4,3,2,1,0:T(8,128)S(1)}, f32[3,2,16,128]{3,2,1,0:T(8,128)S(1)}, f32[3,2,16,128]{3,2,1,0:T(8,128)S(1)}, f32[3,128,128]{2,1,0:T(8,128)S(1)}) custom-call(s32[128]{0:T(128)S(1)} %select_reduce_fusion.sorting_ref, s32[128]{0:T(128)S(1)} %copy-done, s32[4,1,256]{2,1,0:T(1,128)S(1)} %bitcast.5, f32[3,128,128]{2,1,0:T(8,128)} %bitcast.7, ...), custom_call_target="tpu_custom_call" | custom-call | tf_op jit(solution)/shard_map/elements/pallas_call | solution.py:533
  27.2 3.6 %yzpass.1 = (f32[3,2,4,16,512]{4,3,2,1,0:T(8,128)}, f32[3,128,128]{2,1,0:T(8,128)}) custom-call(s32[128]{0:T(128)S(1)} %get-tuple-element.15.position_ref, f32[3,2,4,16,512]{4,3,2,1,0:T(8,128)S(1)} %get-tuple-element.8.field_ref, f32[3,2,16,128]{3,2,1,0:T(8,128)S(1)} %get-tuple-element.9.far_lo_ref, f32[3,2,16,128]{3,2,1,0:T(8,128)S(1)} %get-tuple-element.10.far_hi_ref, ...), custom_call_target="tpu_custom_call" | custom-call | tf_op jit(solution)/shard_map/yzpass/pallas_call | solution.py:646
  (1 shorter events, 0.0 us)
Async XLA Ops:
  0.6 0.7 %copy-start.2 = (s32[128]{0:T(128)S(1)}, s32[128]{0:T(128)}, u32[]{:S(2)}) copy-start(s32[128]{0:T(128)} %param.12) | copy-start | bytes 1540
  1.3 0.7 %copy-start.1 = (s32[128]{0:T(128)S(1)}, s32[128]{0:T(128)}, u32[]{:S(2)}) copy-start(s32[128]{0:T(128)} %param.13) | copy-start | bytes 1540
  2.3 0.7 %copy-start = (s32[128]{0:T(128)S(1)}, s32[128]{0:T(128)}, u32[]{:S(2)}) copy-start(s32[128]{0:T(128)} %count_ref.1) | copy-start | bytes 1540

commit v3 on v2

--- a/solution.py
+++ b/solution.py
@@ -85,11 +85,11 @@
     return jnp.concatenate(refs, axis=0)
 
 
-def project(left, high, low):
+def project(left, both_planes):
     top, rest = split(left)
     both = jnp.concatenate([jnp.concatenate([top, top], axis=1), jnp.concatenate([rest, rest], axis=1)], axis=0)
     out = lax.dot_general(
-        both, jnp.concatenate([high, low], axis=1), (((1,), (1,)), ((), ())), preferred_element_type=jnp.float32
+        both, both_planes, (((1,), (1,)), ((), ())), preferred_element_type=jnp.float32
     )
     return out[: left.shape[0]] + out[left.shape[0] :]
 
@@ -108,11 +108,11 @@
 
 def main_kernel(
     shape, n_gx, n_gy,
-    sorting_ref, count_ref, label_ref, pos_hbm, vel_hbm, coef_hbm, velocity_hbm,
-    field_ref, far_lo_ref, far_hi_ref, ret_ref,
+    position_ref, sorting_ref, count_ref, label_ref, pos_hbm, vel_hbm, coef_hbm, velocity_hbm,
+    field_ref, final_ref,
     pos_in, vel_in, coef_in, vel_ref, send_pos, send_rest, got_pos, got_rest, got_label, slot_row, tag_s, slot_s,
     vs_ref, fluid_ref, drag_ref, dep_ref, ts_ref, fs_ref,
-    pos_ref, gpos_ref, out_ref, gdrag_ref, face_ref, gface_ref, lo_ref, hi_ref,
+    pos_ref, gpos_ref, out_ref, gdrag_ref, face_ref, gface_ref, lo_ref, hi_ref, ret_ref, weight_ref, plane_ref, far_lo_ref, far_hi_ref,
     in_sem, label_sem, block_sem, rest_sem, tag_sem, pos_sem, drag_sem, face_sem, y_sem, back_sem,
 ):
     exd, eyd, ez = shape
@@ -214,6 +214,12 @@
 
         lax.fori_loop(0, share // 8, some, 0)
 
+    for side in range(2):
+        @pl.when(jnp.logical_not(has[side]))
+        def _():
+            gpos_ref[side] = jnp.zeros(gpos_ref.shape[1:], jnp.float32)
+            gdrag_ref[side] = jnp.zeros(gdrag_ref.shape[1:], jnp.float32)
+
     got_label[gy] = label_ref[gy]
     tag_copy(gy, 0).start()
     order = tuple(range(near, n_gy)) + tuple(range(1, near))
@@ -229,7 +235,6 @@
     inputs[2].wait()
     for m in order[: n_gy - near]:
         pack_rest(send_rest, partner(m))
-        rest_copy(m).start()
     for m in order[n_gy - near :]:
         pack_pos(send_pos, partner(m))
         pos_copy(m).start()
@@ -258,31 +263,36 @@
 
         lax.fori_loop(0, count // 8, some, 0)
 
+    slot_copy = pltpu.make_async_copy(slot_row, slot_s, tag_sem.at[n_gy])
+
     def interpolate(index, carry):
-        for m in range(1, near):
-            @pl.when(index == m * per)
-            def _():
+        @pl.when(index == per)
+        def _():
+            for m in order:
                 label_copy(m).wait()
-                tag_copy(partner(m), m).start()
-                pos_copy(m).wait()
-                tag_copy(partner(m), m).wait()
-
-        @pl.when(index == near * per)
-        def _():
-            for m in range(near, n_gy):
-                label_copy(m).wait()
-                tag_copy(partner(m), m).start()
             total = got_label[0]
             for other in range(1, n_gy):
                 total = total + got_label[other]
             slot_row[...] = total[:, 128:]
-            copy = pltpu.make_async_copy(slot_row, slot_s, tag_sem.at[n_gy])
-            copy.start()
+            slot_copy.start()
+            for m in order:
+                tag_copy(partner(m), m).start()
             for m in range(near, n_gy):
+                pos_copy(m).wait_send()
+                rest_copy(m).start()
+            slot_copy.wait()
+            for m in order:
                 tag_copy(partner(m), m).wait()
-            copy.wait()
+
+        for m in range(1, near):
+            @pl.when(index == m * per)
+            def _():
+                pos_copy(m).wait()
+
+        @pl.when(index == near * per)
+        def _():
             for m in range(near, n_gy):
-                pos_copy(m).wait()
+                pos_copy(m).wait_recv()
             collect(pos_ref, got_pos, 0, columns)
             for side in range(2):
                 @pl.when(has[side])
@@ -335,6 +345,18 @@
         at = pl.ds(pl.multiple_of(y * ez, 8), ez)
         return make(side, out_ref.at[side, :, at], gdrag_ref.at[1 - side, :, at], drag_sem, y)
 
+    def strip_start(k):
+        for side in range(2):
+            @pl.when(has[side])
+            def _():
+                drag_copy(to_side, side, k * (eyd - 1) % eyd).start()
+
+    def strip_sent(k):
+        for side in range(2):
+            @pl.when(has[side])
+            def _():
+                drag_copy(to_side, side, k * (eyd - 1) % eyd).wait_send()
+
     def deposit(index, carry):
         @pl.when(index == 0)
         def _():
@@ -347,13 +369,9 @@
             for m in range(near, n_gy):
                 rest_copy(m).wait()
             forces(near * share, elems - near * share)
+            collect(out_ref, drag_ref, 0, columns)
             for k in range(eyd):
-                y = k * (eyd - 1) % eyd
-                collect(out_ref, drag_ref, y * ez, ez)
-                for side in range(2):
-                    @pl.when(has[side])
-                    def _():
-                        drag_copy(to_side, side, y).start()
+                strip_start(k)
             for m in order:
                 back_copy(m).start()
             ret_ref[:, part(gy), :] = drag_ref[:, part(gy), :]
@@ -369,7 +387,7 @@
             weights = (gauss(r, nodes), gauss(r + shift, nodes))
             force = [-line(drag_ref, c, slot) for c in range(3)]
             left = jnp.concatenate([f * w for w in weights for f in force], axis=0)
-            out = project(left, *st_planes(s, t, nodes))
+            out = project(left, jnp.concatenate(st_planes(s, t, nodes), axis=1))
             dep_ref[pl.ds(pl.multiple_of(slot * 2 * ROWS, 8), 2 * ROWS), 0:64] = out
         return carry
 
@@ -413,24 +431,46 @@
         def _():
             from_side(side, pos_ref.at[side], gpos_ref.at[side], pos_sem).wait()
 
+    def prepare(k, carry):
+        for side in range(2):
+            for g in range(8):
+                col = k * 8 + g
+                r, s, t = (jnp.broadcast_to(gpos_ref[side, d, pl.ds(col, 1), :], (8, 128)) * WIDTH for d in range(3))
+                weight_ref[side, col] = gauss(r + (-2.0 if side == 0 else 2.0) * WIDTH, nodes)
+                plane_ref[side, col] = jnp.concatenate(st_planes(s, t, nodes), axis=1)
+        return carry
+
+    lax.fori_loop(0, columns // 8, prepare, 0)
+
+    def pick(i, carry):
+        at = pl.multiple_of(i * 8, 8)
+        spots = [position_ref[at + u] for u in range(8)]
+        for c in range(3):
+            final_ref[c, pl.ds(at, 8), :] = rows_of([line(ret_ref, c, spot) for spot in spots])
+        return carry
+
+    for m in order:
+        back_copy(m).wait()
+    lax.fori_loop(0, elems // 8, pick, 0)
+
     def ghost(k, carry):
         y = strip(k)
+        at = pl.ds(pl.multiple_of(y * ez, 8), ez)
         for side in range(2):
             @pl.when(has[side])
             def _():
-                at = pl.ds(pl.multiple_of(y * ez, 8), ez)
-                from_side(side, out_ref.at[side, :, at], gdrag_ref.at[side, :, at], drag_sem, y).wait()
-                sums = []
-                for g in range(ez):
-                    col = y * ez + g
-                    r, s, t = (jnp.broadcast_to(gpos_ref[side, d, pl.ds(col, 1), :], (8, 128)) * WIDTH for d in range(3))
-                    weight = gauss(r + (-2.0 if side == 0 else 2.0) * WIDTH, nodes)
-                    left = jnp.concatenate([(-gdrag_ref[side, c, pl.ds(col, 1), :]) * weight for c in range(3)], axis=0)
-                    add = project(left, *st_planes(s, t, nodes))
-                    spot = pl.ds(pl.multiple_of((base[side] + col) * ROWS, 8), ROWS)
-                    sums.append((spot, ts_ref[spot, 0:64] + add))
-                for spot, value in sums:
-                    ts_ref[spot, 0:64] = value
+                from_side(side, out_ref.at[side, :, at], gdrag_ref.at[side, :, at], drag_sem, y).wait_recv()
+        sums = []
+        for side in range(2):
+            for g in range(ez):
+                col = y * ez + g
+                weight = weight_ref[side, col]
+                left = jnp.concatenate([(-gdrag_ref[side, c, pl.ds(col, 1), :]) * weight for c in range(3)], axis=0)
+                add = project(left, plane_ref[side, col])
+                spot = pl.ds(pl.multiple_of((base[side] + col) * ROWS, 8), ROWS)
+                sums.append((spot, ts_ref[spot, 0:64] + add))
+        for spot, value in sums:
+            ts_ref[spot, 0:64] = value
         return carry
 
     lax.fori_loop(0, eyd, ghost, 0)
@@ -442,6 +482,9 @@
 
     low = lane_iota((ez, 128)) < 64
     spot64 = lane_iota((ez, 128)) % 64
+    depth = lax.broadcasted_iota(jnp.int32, (ez, 128), 0)
+    up = (spot64 % 8 == 7) & (depth < ez - 1)
+    down = (spot64 % 8 == 0) & (depth > 0)
     lo_copy = pltpu.make_async_remote_copy(
         src_ref=lo_ref, dst_ref=far_lo_ref, send_sem=y_sem.at[0, 0], recv_sem=y_sem.at[1, 0],
         device_id={"gy": gy - 1}, device_id_type=mesh_id,
@@ -451,18 +494,17 @@
         device_id={"gy": gy + 1}, device_id_type=mesh_id,
     )
 
-    def assemble(index, carry):
-        k, c = lax.div(index, 3), lax.rem(index, 3)
+    def assemble(k, carry):
         y = strip(k)
         upper = y >= eyd // 2
 
-        def lanes(x, q):
+        def lanes(c, x, q):
             start = (x * columns + y * ez) * ROWS + c * 8 + 2 * q
             even = ts_ref[pl.ds(start, ez, stride=ROWS), :]
             odd = ts_ref[pl.ds(start + 1, ez, stride=ROWS), :]
             return jnp.where(low, even, pltpu.roll(odd, 64, 1))
 
-        def far(side):
+        def far(c, side):
             came = gface_ref[side, c, pl.ds(pl.multiple_of(lax.rem(y, eyd // 2) * ez, 8), ez), :]
             turned = pltpu.roll(came, 64, 1)
             came = jnp.where(low != upper, came, turned)
@@ -470,57 +512,93 @@
             mine = jnp.where(low, mine, pltpu.roll(mine, 64, 1))
             return jnp.where(has[side], came + mine, 0.0)
 
-        grid = [[lanes(x, q) for q in range(4)] for x in range(exd)]
-        for x in range(exd):
-            above = pltpu.roll(grid[x + 1][0], 64, 1) if x + 1 < exd else far(1)
-            below = pltpu.roll(grid[x - 1][3], 64, 1) if x > 0 else far(0)
-            done = list(grid[x])
-            done[3] = done[3] + jnp.where(low, 0.0, above)
-            done[0] = done[0] + jnp.where(low, below, 0.0)
-            for q in range(4):
-                field_ref[c, x, y, :, q * 128 : (q + 1) * 128] = done[q]
-
-            @pl.when(k == 0)
-            def _():
+        edges = []
+        for c in range(3):
+            grid = [[lanes(c, x, q) for q in range(4)] for x in range(exd)]
+            for x in range(exd):
+                above = pltpu.roll(grid[x + 1][0], 64, 1) if x + 1 < exd else far(c, 1)
+                below = pltpu.roll(grid[x - 1][3], 64, 1) if x > 0 else far(c, 0)
+                done = list(grid[x])
+                done[3] = done[3] + jnp.where(low, 0.0, above)
+                done[0] = done[0] + jnp.where(low, below, 0.0)
+                for q in range(4):
+                    nxt = pltpu.roll(pltpu.roll(done[q], ez - 1, 0), 7, 1)
+                    prv = pltpu.roll(pltpu.roll(done[q], 1, 0), 121, 1)
+                    done[q] = done[q] + jnp.where(up, nxt, 0.0) + jnp.where(down, prv, 0.0)
+                for q in range(4):
+                    field_ref[c, x, y, :, q * 128 : (q + 1) * 128] = done[q]
+
+                edges.append((c, x, done))
+
+        @pl.when(k == 0)
+        def _():
+            for c, x, done in edges:
                 face = jnp.where(spot64 < 8, done[0], 0.0)
                 for q in range(1, 4):
                     face = face + pltpu.roll(jnp.where(spot64 < 8, done[q], 0.0), 8 * q, 1)
                 lo_ref[c, x] = face
 
-            @pl.when(k == 1)
+            @pl.when(gy > 0)
             def _():
+                lo_copy.start()
+
+        @pl.when(k == 1)
+        def _():
+            for c, x, done in edges:
                 face = jnp.where(spot64 >= 56, done[0], 0.0)
                 for q in range(1, 4):
                     face = face + pltpu.roll(jnp.where(spot64 >= 56, done[q], 0.0), 128 - 8 * q, 1)
                 hi_ref[c, x] = face
 
-        @pl.when((index == 2) & (gy > 0))
-        def _():
-            lo_copy.start()
-
-        @pl.when((index == 5) & (gy < n_gy - 1))
-        def _():
-            hi_copy.start()
+            @pl.when(gy < n_gy - 1)
+            def _():
+                hi_copy.start()
 
         return carry
 
-    lax.fori_loop(0, 3 * eyd, assemble, 0)
+    lax.fori_loop(0, eyd, assemble, 0)
+
+    def across(c, carry):
+        for x in range(exd):
+            for q in range(4):
+                spot = slice(q * 128, (q + 1) * 128)
+                cells = [field_ref[c, x, y, :, spot] for y in range(eyd)]
+                for y in range(eyd):
+                    v = cells[y]
+                    if y + 1 < eyd:
+                        v = v + jnp.where(spot64 >= 56, pltpu.roll(cells[y + 1], 56, 1), 0.0)
+                    if y > 0:
+                        v = v + jnp.where(spot64 < 8, pltpu.roll(cells[y - 1], 72, 1), 0.0)
+                    field_ref[c, x, y, :, spot] = v
+        return carry
+
+    lax.fori_loop(0, 3, across, 0)
+    for k in range(eyd):
+        strip_sent(k)
+
+    def edge(far_ref, y, keep, turn):
+        for c in range(3):
+            for x in range(exd):
+                far_edge = far_ref[c, x]
+                for q in range(4):
+                    spot = slice(q * 128, (q + 1) * 128)
+                    add = jnp.where(keep, pltpu.roll(far_edge, turn(q) % 128, 1), 0.0)
+                    field_ref[c, x, y, :, spot] = field_ref[c, x, y, :, spot] + add
 
     @pl.when(gy > 0)
     def _():
+        hi_copy.wait_recv()
+        edge(far_hi_ref, 0, spot64 < 8, lambda q: 72 + 8 * q)
         lo_copy.wait_send()
-        hi_copy.wait_recv()
 
     @pl.when(gy < n_gy - 1)
     def _():
+        lo_copy.wait_recv()
+        edge(far_lo_ref, eyd - 1, spot64 >= 56, lambda q: 56 - 8 * q)
         hi_copy.wait_send()
-        lo_copy.wait_recv()
-
-    for m in order:
-        back_copy(m).wait()
-
-
-def run_main(sorting, counts, label, pos, vel, coef, velocity, shape):
+
+
+def run_main(position, sorting, counts, label, pos, vel, coef, velocity, shape):
     exd, eyd, ez = shape
     elems = exd * eyd * ez
     columns = eyd * ez
@@ -534,14 +612,12 @@
         functools.partial(main_kernel, shape, n_gx, n_gy),
         out_shape=(
             jax.ShapeDtypeStruct((3, exd, eyd, ez, 512), f32),
-            jax.ShapeDtypeStruct(face, f32),
-            jax.ShapeDtypeStruct(face, f32),
             jax.ShapeDtypeStruct((3, elems, 128), f32),
         ),
-        in_specs=[pl.BlockSpec(memory_space=SMEM)] * 2
+        in_specs=[pl.BlockSpec(memory_space=SMEM)] * 3
         + [pl.BlockSpec(memory_space=VMEM)]
         + [pl.BlockSpec(memory_space=pltpu.HBM)] * 4,
-        out_specs=[pl.BlockSpec(memory_space=VMEM)] * 4,
+        out_specs=[pl.BlockSpec(memory_space=VMEM)] * 2,
         scratch_shapes=[
             pltpu.VMEM(pos.shape, f32),
             pltpu.VMEM(vel.shape, f32),
@@ -569,6 +645,11 @@
             pltpu.VMEM((2, 3, columns // 2, 128), f32),
             pltpu.VMEM(face, f32),
             pltpu.VMEM(face, f32),
+            pltpu.VMEM((3, elems, 128), f32),
+            pltpu.VMEM((2, columns, 8, 128), f32),
+            pltpu.VMEM((2, columns, 64, 256), jnp.bfloat16),
+            pltpu.VMEM(face, f32),
+            pltpu.VMEM(face, f32),
             dma((4,)),
             dma((2, n_gy - 1)),
             dma((2, n_gy - 1)),
@@ -584,74 +665,29 @@
             vmem_limit_bytes=40 * 1024 * 1024, collective_id=0, has_side_effects=True
         ),
         name="elements",
-    )(sorting, counts, label, *hbm)
-
-
-def yz_pass(position_ref, field_ref, far_lo_ref, far_hi_ref, ret_ref, out_ref, drag_ref, buf_ref, sem):
-    _, exd, eyd, ez, _ = field_ref.shape
-    at = lax.axis_index("gy")
-    first = at > 0
-    last = at < lax.axis_size("gy") - 1
-    place = lane_iota((ez, 128)) % 64
-    k = lane_iota((ez, 128)) % 8
-    row = lax.broadcasted_iota(jnp.int32, (ez, 128), 0)
-    up = (k == 7) & (row < ez - 1)
-    down = (k == 0) & (row > 0)
-
-    def out_copy(c, x):
-        return pltpu.make_async_copy(buf_ref.at[c, x], out_ref.at[c, x], sem.at[c, x])
-
-    def layer(index, carry):
-        c, x = lax.div(index, exd), lax.rem(index, exd)
-        far_lo = jnp.where(last, far_lo_ref[c, x], 0.0)
-        far_hi = jnp.where(first, far_hi_ref[c, x], 0.0)
-        for q in range(4):
-            spot = slice(q * 128, (q + 1) * 128)
-            cells = [field_ref[c, x, y, :, spot] for y in range(eyd)]
-            for y in range(eyd):
-                if y + 1 < eyd:
-                    above = pltpu.roll(cells[y + 1], 56, 1)
-                else:
-                    above = pltpu.roll(far_lo, (56 - 8 * q) % 128, 1)
-                if y > 0:
-                    below = pltpu.roll(cells[y - 1], 72, 1)
-                else:
-                    below = pltpu.roll(far_hi, (72 + 8 * q) % 128, 1)
-                v = cells[y] + jnp.where(place >= 56, above, 0.0) + jnp.where(place < 8, below, 0.0)
-                nxt = pltpu.roll(pltpu.roll(v, ez - 1, 0), 7, 1)
-                prv = pltpu.roll(pltpu.roll(v, 1, 0), 121, 1)
-                buf_ref[c, x, y, :, spot] = v + jnp.where(up, nxt, 0.0) + jnp.where(down, prv, 0.0)
-        out_copy(c, x).start()
-        return carry
-
-    lax.fori_loop(0, 3 * exd, layer, 0)
-
-    def pick(index, carry):
-        spots = [position_ref[index * 8 + u] for u in range(8)]
-        for c in range(3):
-            drag_ref[c, pl.ds(pl.multiple_of(index * 8, 8), 8), :] = rows_of([line(ret_ref, c, at) for at in spots])
-        return carry
-
-    lax.fori_loop(0, ret_ref.shape[1] // 8, pick, 0)
-
-    def drain(index, carry):
-        out_copy(lax.div(index, exd), lax.rem(index, exd)).wait()
-        return carry
-
-    lax.fori_loop(0, 3 * exd, drain, 0)
-
-
-def run_yz(position, field, far_lo, far_hi, ret):
+    )(position, sorting, counts, label, *hbm)
+
+
+def store_pass(field_ref, final_ref, out_ref, drag_ref, sem):
+    copies = [pltpu.make_async_copy(field_ref.at[c], out_ref.at[c], sem.at[c]) for c in range(3)]
+    copies.append(pltpu.make_async_copy(final_ref, drag_ref, sem.at[3]))
+    for copy in copies:
+        copy.start()
+    for copy in copies:
+        copy.wait()
+
+
+def run_store(field, final):
     f32 = jnp.float32
     return pl.pallas_call(
-        yz_pass,
-        out_shape=(jax.ShapeDtypeStruct(field.shape, f32), jax.ShapeDtypeStruct(ret.shape, f32)),
-        in_specs=[pl.BlockSpec(memory_space=SMEM)] + [pl.BlockSpec(memory_space=VMEM)] * 4,
-        out_specs=[pl.BlockSpec(memory_space=pl.ANY), pl.BlockSpec(memory_space=VMEM)],
-        scratch_shapes=[pltpu.VMEM(field.shape, f32), pltpu.SemaphoreType.DMA(field.shape[:2])],
+        store_pass,
+        out_shape=(jax.ShapeDtypeStruct(field.shape, f32), jax.ShapeDtypeStruct(final.shape, f32)),
+        in_specs=[pl.BlockSpec(memory_space=VMEM)] * 2,
+        out_specs=[pl.BlockSpec(memory_space=pl.ANY)] * 2,
+        scratch_shapes=[pltpu.SemaphoreType.DMA((4,))],
         compiler_params=pltpu.CompilerParams(vmem_limit_bytes=32 * 1024 * 1024),
-        name="yzpass",
-    )(position, field, far_lo, far_hi, ret)
+        name="store",
+    )(field, final)
 
 
 def inverse_of(position):
@@ -676,11 +712,11 @@
         cells == (dest * 256 + 128 + elem)[None, :], (lax.axis_index("gy") * share + rank)[None, :], 0
     )
     label = jnp.sum(tags + slots, axis=1).reshape(devices, 1, 256)
-    field, far_lo, far_hi, ret = run_main(
-        sorting, counts, label, part_pos.transpose(1, 0, 2), part_vel.transpose(1, 0, 2), part_coef,
+    field, final = run_main(
+        position, sorting, counts, label, part_pos.transpose(1, 0, 2), part_vel.transpose(1, 0, 2), part_coef,
         velocity.reshape(3, elems, nodes), (exd, eyd, ez),
     )
-    source, drag_out = run_yz(position, field, far_lo, far_hi, ret)
+    source, drag_out = run_store(field, final)
     return (drag_out.transpose(1, 0, 2), source)
 
 

time: 31.4 us -> 28.1 us (0.89); the launches traced: 30.8 us -> 27.9 us
  Pallas kernels: 27.9 us -> 25 us
    pallas_call x1, Pallas kernels: 3.61 us -> 0.97 us  [run_store(): pl.pallas_call(store_pass, out_shape=(jax.ShapeDtypeStruct(field.shape, f...]
where the time goes in v3:
time: 28.1 us; the launch traced here: 27.9 us
  Pallas kernels  25 us (89%)
  local copies, waits for them, and re-layouts  1.78 us (6%)
  between operations  0.67 us (2%)
  other arithmetic  0.5 us (2%)
    pallas_call x1, Pallas kernels, run_main(): pl.pallas_call(functools.partial(main_kernel, shape, n_gx, n_gy), out_sha...  24 us
    unnamed x6, local copies, waits for them, and re-layouts  1.78 us
    pallas_call x1, Pallas kernels, run_store(): pl.pallas_call(store_pass, out_shape=(jax.ShapeDtypeStruct(field.shape, f...  0.97 us

profile of v3, /device:TPU:9, one launch (start us, length us, event | category | flops | bytes accessed | tf_op | source)
XLA Modules:
  0.0 27.9 jit_solution(2378854455780201369)
XLA Ops:
  0.6 0.0 copy-start.2
  0.6 0.6 %copy-done.2 = s32[128]{0:T(128)S(1)} copy-done((s32[128]{0:T(128)S(1)}, s32[128]{0:T(128)}, u32[]{:S(2)}) %copy-start.2) | copy-done | bytes 536
  1.3 0.0 copy-start.1
  1.3 0.2 convert_reduce_fusion
  1.5 0.5 %copy-done.1 = s32[128]{0:T(128)S(1)} copy-done((s32[128]{0:T(128)S(1)}, s32[128]{0:T(128)}, u32[]{:S(2)}) %copy-start.1) | copy-done | bytes 536
  2.0 0.1 select_reduce_fusion.sorting_ref
  2.1 0.2 add_reduce_fusion
  2.3 0.0 copy-start
  2.3 0.6 %copy-done = s32[128]{0:T(128)S(1)} copy-done((s32[128]{0:T(128)S(1)}, s32[128]{0:T(128)}, u32[]{:S(2)}) %copy-start) | copy-done | bytes 536
  2.9 24.0 %elements.1 = (f32[3,2,4,16,512]{4,3,2,1,0:T(8,128)S(1)}, f32[3,128,128]{2,1,0:T(8,128)S(1)}) custom-call(s32[128]{0:T(128)S(1)} %get-tuple-element.11.position_ref, s32[128]{0:T(128)S(1)} %select_reduce_fusion.sorting_ref, s32[128]{0:T(128)S(1)} %copy-done, s32[4,1,256]{2,1,0:T(1,128)S(1)} %bitcast.5, f32[3,128,128]{2,1,0:T(8,128)} %bitcast.7, ...), custom_call_target="tpu_custom_call" | custom-call | tf_op jit(solution)/shard_map/elements/pallas_call | solution.py:611
  27.0 1.0 %store.1 = (f32[3,2,4,16,512]{4,3,2,1,0:T(8,128)}, f32[3,128,128]{2,1,0:T(8,128)}) custom-call(f32[3,2,4,16,512]{4,3,2,1,0:T(8,128)S(1)} %get-tuple-element.6.field_ref, f32[3,128,128]{2,1,0:T(8,128)S(1)} %get-tuple-element.7.final_ref), custom_call_target="tpu_custom_call" | custom-call | tf_op jit(solution)/shard_map/store/pallas_call | solution.py:682
  (1 shorter events, 0.0 us)
Async XLA Ops:
  0.6 0.7 %copy-start.2 = (s32[128]{0:T(128)S(1)}, s32[128]{0:T(128)}, u32[]{:S(2)}) copy-start(s32[128]{0:T(128)} %param.12) | copy-start | bytes 1540
  1.3 0.7 %copy-start.1 = (s32[128]{0:T(128)S(1)}, s32[128]{0:T(128)}, u32[]{:S(2)}) copy-start(s32[128]{0:T(128)} %param.13) | copy-start | bytes 1540
  2.3 0.7 %copy-start = (s32[128]{0:T(128)S(1)}, s32[128]{0:T(128)}, u32[]{:S(2)}) copy-start(s32[128]{0:T(128)} %count_ref.1) | copy-start | bytes 1540

commit v4 on v3

--- a/solution.py
+++ b/solution.py
@@ -108,9 +108,9 @@
 
 def main_kernel(
     shape, n_gx, n_gy,
-    position_ref, sorting_ref, count_ref, label_ref, pos_hbm, vel_hbm, coef_hbm, velocity_hbm,
+    dest_hbm, elem_hbm, count_hbm, pos_hbm, vel_hbm, coef_hbm, velocity_hbm,
     field_ref, final_ref,
-    pos_in, vel_in, coef_in, vel_ref, send_pos, send_rest, got_pos, got_rest, got_label, slot_row, tag_s, slot_s,
+    dest_in, elem_in, count_in, pos_in, vel_in, coef_in, vel_ref, label_ref, place_row, position_ref, send_pos, send_rest, got_pos, got_rest, got_label, slot_row, tag_s, slot_s,
     vs_ref, fluid_ref, drag_ref, dep_ref, ts_ref, fs_ref,
     pos_ref, gpos_ref, out_ref, gdrag_ref, face_ref, gface_ref, lo_ref, hi_ref, ret_ref, weight_ref, plane_ref, far_lo_ref, far_hi_ref,
     in_sem, label_sem, block_sem, rest_sem, tag_sem, pos_sem, drag_sem, face_sem, y_sem, back_sem,
@@ -136,7 +136,10 @@
             bit *= 2
         return total
 
-    pairs = ((pos_hbm, pos_in), (vel_hbm, vel_in), (coef_hbm, coef_in), (velocity_hbm, vel_ref))
+    pairs = (
+        (dest_hbm, dest_in), (elem_hbm, elem_in), (count_hbm, count_in),
+        (pos_hbm, pos_in), (vel_hbm, vel_in), (coef_hbm, coef_in), (velocity_hbm, vel_ref),
+    )
     inputs = [pltpu.make_async_copy(src, dst, in_sem.at[i]) for i, (src, dst) in enumerate(pairs)]
     for copy in inputs:
         copy.start()
@@ -188,69 +191,98 @@
     def tag_copy(index, m):
         return pltpu.make_async_copy(got_label.at[index], tag_s.at[index], tag_sem.at[m])
 
-    lane = lane_iota((1, 128))
-
-    def pack_pos(dst, index):
-        def some(i, carry):
-            start = pl.multiple_of(index * share + i * 8, 8)
-            spots = [sorting_ref[start + u] for u in range(8)]
-            for c in range(3):
-                dst[c, pl.ds(start, 8), :] = rows_of([line(pos_in, c, b) for b in spots])
-            return carry
-
-        lax.fori_loop(0, share // 8, some, 0)
-
-    def pack_rest(dst, index):
-        def some(i, carry):
-            start = pl.multiple_of(index * share + i * 8, 8)
-            spots = [sorting_ref[start + u] for u in range(8)]
-            for c in range(3):
-                dst[c, pl.ds(start, 8), :] = rows_of([line(vel_in, c, b) for b in spots])
-            dst[3, pl.ds(start, 8), :] = rows_of(
-                [jnp.where(lane < count_ref[b], coef_in[b, 0:1, :], 0.0) for b in spots]
-            )
-            dst[4, pl.ds(start, 8), :] = rows_of([coef_in[b, 1:2, :] for b in spots])
-            return carry
-
-        lax.fori_loop(0, share // 8, some, 0)
-
     for side in range(2):
         @pl.when(jnp.logical_not(has[side]))
         def _():
             gpos_ref[side] = jnp.zeros(gpos_ref.shape[1:], jnp.float32)
             gdrag_ref[side] = jnp.zeros(gdrag_ref.shape[1:], jnp.float32)
 
-    got_label[gy] = label_ref[gy]
-    tag_copy(gy, 0).start()
+    f32, bf16 = jnp.float32, jnp.bfloat16
+    across_lanes = (((1,), (1,)), ((), ()))
+    height = lax.broadcasted_iota(i32, (elems, elems), 0)
+    for copy in inputs[:3]:
+        copy.wait()
+    dest_row, elem_row = dest_in[...], elem_in[...]
+    square = (elems, elems)
+    wide = lane_iota(square)
+
+    def turned(x):
+        return jnp.broadcast_to(x, square).T
+
+    def summed(x):
+        while x.shape[0] > 8:
+            x = x[: x.shape[0] // 2] + x[x.shape[0] // 2 :]
+        for step in (4, 2, 1):
+            x = x + pltpu.roll(x, step, 0)
+        return x[0:1]
+
+    dest_col, elem_col = turned(dest_row), turned(elem_row)
+    rank = summed(jnp.where((dest_col == dest_row) & (height < wide), 1, 0))
+    place = dest_row * share + rank
+    place_row[...] = place
+    place_copy = pltpu.make_async_copy(place_row, position_ref, tag_sem.at[n_gy + 1])
+    place_copy.start()
+    chosen = (place == height).astype(bf16)
+    place_col = turned(place)
+    tags = summed(jnp.where(place_col == wide, elem_col, 0))
+    slot_col = place_col + (gy - dest_col) * share
+    slot_col = jnp.where(elem_col == wide, slot_col, 0)
+    for d in range(n_gy):
+        label_ref[d] = jnp.concatenate([tags, summed(jnp.where(dest_col == d, slot_col, 0))], axis=1)
+
+    def in_order(x):
+        top = x.astype(bf16)
+        left = x - top.astype(f32)
+        middle = left.astype(bf16)
+        bottom = (left - middle.astype(f32)).astype(bf16)
+        return (
+            jnp.dot(chosen, top, preferred_element_type=f32)
+            + jnp.dot(chosen, middle, preferred_element_type=f32)
+            + jnp.dot(chosen, bottom, preferred_element_type=f32)
+        )
+
     order = tuple(range(near, n_gy)) + tuple(range(1, near))
-    inputs[0].wait()
-    for m in order[: n_gy - near]:
-        pack_pos(send_pos, partner(m))
+    inputs[3].wait()
+    both = in_order(jnp.concatenate([pos_in[0], pos_in[1]], axis=1))
+    send_pos[0] = both[:, :128]
+    send_pos[1] = both[:, 128:]
+    send_pos[2] = in_order(pos_in[2])
     pl.semaphore_wait(barrier, n_gy - 1 + has[0].astype(i32) + has[1].astype(i32))
     for m in order:
         label_copy(m).start()
-    for m in order[: n_gy - near]:
+    for m in order:
         pos_copy(m).start()
-    inputs[1].wait()
-    inputs[2].wait()
-    for m in order[: n_gy - near]:
-        pack_rest(send_rest, partner(m))
-    for m in order[n_gy - near :]:
-        pack_pos(send_pos, partner(m))
-        pos_copy(m).start()
-        pack_rest(send_rest, partner(m))
+    got_label[gy] = label_ref[gy]
+    tag_copy(gy, 0).start()
+    got_pos[:, part(gy), :] = send_pos[:, part(gy), :]
+    inputs[4].wait()
+    inputs[5].wait()
+    both = in_order(jnp.concatenate([vel_in[0], vel_in[1]], axis=1))
+    send_rest[0] = both[:, :128]
+    send_rest[1] = both[:, 128:]
+    both = in_order(jnp.concatenate([vel_in[2], coef_in[pl.ds(0, elems, stride=2), :]], axis=1))
+    live = lax.dot_general(
+        chosen, jnp.broadcast_to(count_in[...].astype(f32), (128, elems)).astype(bf16), across_lanes,
+        preferred_element_type=f32,
+    )
+    send_rest[2] = both[:, :128]
+    send_rest[3] = jnp.where(lane_iota((elems, 128)).astype(f32) < live, both[:, 128:], 0.0)
+    send_rest[4] = in_order(coef_in[pl.ds(1, elems, stride=2), :])
+    for m in range(1, near):
         rest_copy(m).start()
-    pack_pos(got_pos, gy)
-    pack_rest(got_rest, gy)
-    inputs[3].wait()
+    got_rest[:, part(gy), :] = send_rest[:, part(gy), :]
+    inputs[6].wait()
     spread_nodes(vel_ref, vs_ref, elems)
     consts = node_consts()
     nodes, others, scale = consts
     nodes = nodes * WIDTH
     tag_copy(gy, 0).wait()
 
+    def within(i):
+        return jnp.minimum(jnp.maximum(i, 0), elems - 1)
+
     def slot_of(e):
-        return slot_s[0, e]
+        return within(slot_s[0, e])
 
     def collect(dst, src, start, count):
         def some(i, carry):
@@ -306,7 +338,7 @@
             for u in range(8):
                 i = first + batch * 8 + u
                 slot = source * share + i
-                e = tag_s[source, 0, i]
+                e = within(tag_s[source, 0, gy * share + i])
                 r, s, t = (wide_line(got_pos, d, slot) for d in range(3))
                 basis_r = lagrange(r, others, scale)
                 high, low = split(planes(lagrange(s, others, scale), lagrange(t, others, scale)))
@@ -381,7 +413,7 @@
         for u in range(group):
             i = first + u
             slot = source * share + i
-            layer = jnp.full((8, 128), tag_s[source, 0, i], i32)
+            layer = jnp.full((8, 128), tag_s[source, 0, gy * share + i], i32)
             shift = jnp.where(layer < columns, -2.0 * WIDTH, 2.0 * WIDTH)
             r, s, t = (wide_line(got_pos, d, slot) * WIDTH for d in range(3))
             weights = (gauss(r, nodes), gauss(r + shift, nodes))
@@ -444,11 +476,12 @@
 
     def pick(i, carry):
         at = pl.multiple_of(i * 8, 8)
-        spots = [position_ref[at + u] for u in range(8)]
+        spots = [within(position_ref[0, at + u]) for u in range(8)]
         for c in range(3):
             final_ref[c, pl.ds(at, 8), :] = rows_of([line(ret_ref, c, spot) for spot in spots])
         return carry
 
+    place_copy.wait()
     for m in order:
         back_copy(m).wait()
     lax.fori_loop(0, elems // 8, pick, 0)
@@ -598,7 +631,7 @@
         hi_copy.wait_send()
 
 
-def run_main(position, sorting, counts, label, pos, vel, coef, velocity, shape):
+def run_main(arrays, shape):
     exd, eyd, ez = shape
     elems = exd * eyd * ez
     columns = eyd * ez
@@ -606,30 +639,29 @@
     f32, i32 = jnp.float32, jnp.int32
     dma = pltpu.SemaphoreType.DMA
     face = (3, exd, ez, 128)
+    label = (n_gy, 1, 2 * elems)
     strips = (2, 3, columns, 128)
-    hbm = [pltpu.with_memory_space_constraint(x, pltpu.HBM) for x in (pos, vel, coef, velocity)]
+    hbm = [pltpu.with_memory_space_constraint(x, pltpu.HBM) for x in arrays]
     return pl.pallas_call(
         functools.partial(main_kernel, shape, n_gx, n_gy),
         out_shape=(
             jax.ShapeDtypeStruct((3, exd, eyd, ez, 512), f32),
             jax.ShapeDtypeStruct((3, elems, 128), f32),
         ),
-        in_specs=[pl.BlockSpec(memory_space=SMEM)] * 3
-        + [pl.BlockSpec(memory_space=VMEM)]
-        + [pl.BlockSpec(memory_space=pltpu.HBM)] * 4,
+        in_specs=[pl.BlockSpec(memory_space=pltpu.HBM)] * len(hbm),
         out_specs=[pl.BlockSpec(memory_space=VMEM)] * 2,
         scratch_shapes=[
-            pltpu.VMEM(pos.shape, f32),
-            pltpu.VMEM(vel.shape, f32),
-            pltpu.VMEM(coef.shape, f32),
-            pltpu.VMEM(velocity.shape, velocity.dtype),
+            *(pltpu.VMEM(x.shape, x.dtype) for x in arrays),
+            pltpu.VMEM(label, i32),
+            pltpu.VMEM((1, elems), i32),
+            pltpu.SMEM((1, elems), i32),
             pltpu.VMEM((3, elems, 128), f32),
             pltpu.VMEM((5, elems, 128), f32),
             pltpu.VMEM((3, elems, 128), f32),
             pltpu.VMEM((5, elems, 128), f32),
-            pltpu.VMEM(label.shape, i32),
+            pltpu.VMEM(label, i32),
             pltpu.VMEM((1, 128), i32),
-            pltpu.SMEM(label.shape, i32),
+            pltpu.SMEM(label, i32),
             pltpu.SMEM((1, 128), i32),
             pltpu.VMEM((elems * ROWS, 128), f32),
             pltpu.VMEM((3, elems, 128), f32),
@@ -650,11 +682,11 @@
             pltpu.VMEM((2, columns, 64, 256), jnp.bfloat16),
             pltpu.VMEM(face, f32),
             pltpu.VMEM(face, f32),
-            dma((4,)),
+            dma((len(hbm),)),
             dma((2, n_gy - 1)),
             dma((2, n_gy - 1)),
             dma((2, n_gy - 1)),
-            dma((n_gy + 1,)),
+            dma((n_gy + 2,)),
             dma((2, 2)),
             dma((2, 2, eyd)),
             dma((2, 2)),
@@ -665,7 +697,7 @@
             vmem_limit_bytes=40 * 1024 * 1024, collective_id=0, has_side_effects=True
         ),
         name="elements",
-    )(position, sorting, counts, label, *hbm)
+    )(*hbm)
 
 
 def store_pass(field_ref, final_ref, out_ref, drag_ref, sem):
@@ -690,33 +722,15 @@
     )(field, final)
 
 
-def inverse_of(position):
-    n = position.shape[0]
-    ladder = jnp.arange(n, dtype=jnp.int32)
-    return jnp.sum(jnp.where(position[None, :] == ladder[:, None], ladder[None, :], 0), axis=1)
-
-
 def body(velocity, part_pos, part_vel, part_coef, counts, dest, elem):
     _, exd, eyd, ez, nodes = velocity.shape
     elems = exd * eyd * ez
-    devices = lax.axis_size("gy")
-    share = elems // devices
-    ladder = jnp.arange(elems, dtype=jnp.int32)
-    earlier = (dest[None, :] == dest[:, None]) & (ladder[None, :] < ladder[:, None])
-    rank = jnp.sum(earlier.astype(jnp.int32), axis=1)
-    position = dest * share + rank
-    sorting = inverse_of(position)
-    cells = jnp.arange(devices * 256, dtype=jnp.int32)[:, None]
-    tags = jnp.where(cells == (dest * 256 + rank)[None, :], elem[None, :], 0)
-    slots = jnp.where(
-        cells == (dest * 256 + 128 + elem)[None, :], (lax.axis_index("gy") * share + rank)[None, :], 0
+    arrays = (
+        dest.reshape(1, elems), elem.reshape(1, elems), counts.reshape(1, elems),
+        part_pos.transpose(1, 0, 2), part_vel.transpose(1, 0, 2), part_coef.reshape(2 * elems, 128),
+        velocity.reshape(3, elems, nodes),
     )
-    label = jnp.sum(tags + slots, axis=1).reshape(devices, 1, 256)
-    field, final = run_main(
-        position, sorting, counts, label, part_pos.transpose(1, 0, 2), part_vel.transpose(1, 0, 2), part_coef,
-        velocity.reshape(3, elems, nodes), (exd, eyd, ez),
-    )
-    source, drag_out = run_store(field, final)
+    source, drag_out = run_store(*run_main(arrays, (exd, eyd, ez)))
     return (drag_out.transpose(1, 0, 2), source)
 
 

time: 28.1 us -> 25.3 us (0.900)
  local copies, waits for them, and re-layouts: 1.78 us -> 0 us
  Pallas kernels: 25 us -> 24.5 us
  other arithmetic: 0.5 us -> 0 us
    unnamed x6 -> x0, local copies, waits for them, and re-layouts: 1.78 us -> none
    reduce_sum x3 -> x0, other arithmetic: 0.49 us -> none  [the longest x1 0.22 us: body(): label = jnp.sum(tags + slots, axis=1).reshape(devices, 1, 256)]
    pallas_call x1, Pallas kernels: 24 us -> 23.6 us  [run_main(): pl.pallas_call(functools.partial(main_kernel, shape, n_gx, n_gy), out_sha...]
where the time goes in v4:
time: 25.3 us; the launch traced here: 25.2 us
  Pallas kernels  24.5 us (97%)
  between operations  0.64 us (3%)
    pallas_call x1, Pallas kernels, run_main(): pl.pallas_call(functools.partial(main_kernel, shape, n_gx, n_gy), out_sha...  23.6 us
    pallas_call x1, Pallas kernels, run_store(): pl.pallas_call(store_pass, out_shape=(jax.ShapeDtypeStruct(field.shape, f...  0.97 us

profile of v4, /device:TPU:9, one launch (start us, length us, event | category | flops | bytes accessed | tf_op | source)
XLA Modules:
  0.0 25.2 jit_solution(4513277963593769312)
XLA Ops:
  0.6 23.6 %elements.1 = (f32[3,2,4,16,512]{4,3,2,1,0:T(8,128)S(1)}, f32[3,128,128]{2,1,0:T(8,128)S(1)}) custom-call(s32[1,128]{1,0:T(1,128)} %bitcast.12, s32[1,128]{1,0:T(1,128)} %bitcast.13, s32[1,128]{1,0:T(1,128)} %bitcast.14, f32[3,128,128]{2,1,0:T(8,128)} %bitcast.9, f32[3,128,128]{2,1,0:T(8,128)} %bitcast.10, f32[256,128]{1,0:T(8,128)} %bitcast.11, ...), custom_call_target="tpu_custom_call" | custom-call | tf_op jit(solution)/shard_map/elements/pallas_call | solution.py:645
  24.2 1.0 %store.1 = (f32[3,2,4,16,512]{4,3,2,1,0:T(8,128)}, f32[3,128,128]{2,1,0:T(8,128)}) custom-call(f32[3,2,4,16,512]{4,3,2,1,0:T(8,128)S(1)} %get-tuple-element.6.field_ref, f32[3,128,128]{2,1,0:T(8,128)S(1)} %get-tuple-element.7.final_ref), custom_call_target="tpu_custom_call" | custom-call | tf_op jit(solution)/shard_map/store/pallas_call | solution.py:714

commit v5 on v4

--- a/solution.py
+++ b/solution.py
@@ -119,7 +119,6 @@
     elems = exd * eyd * ez
     columns = eyd * ez
     share = elems // n_gy
-    half = columns // 2
     group = 16
     per = share // group
     near = n_gy // 2
@@ -230,7 +229,7 @@
     for d in range(n_gy):
         label_ref[d] = jnp.concatenate([tags, summed(jnp.where(dest_col == d, slot_col, 0))], axis=1)
 
-    def in_order(x):
+    def picked(chosen, x):
         top = x.astype(bf16)
         left = x - top.astype(f32)
         middle = left.astype(bf16)
@@ -243,10 +242,10 @@
 
     order = tuple(range(near, n_gy)) + tuple(range(1, near))
     inputs[3].wait()
-    both = in_order(jnp.concatenate([pos_in[0], pos_in[1]], axis=1))
+    both = picked(chosen, jnp.concatenate([pos_in[0], pos_in[1]], axis=1))
     send_pos[0] = both[:, :128]
     send_pos[1] = both[:, 128:]
-    send_pos[2] = in_order(pos_in[2])
+    send_pos[2] = picked(chosen, pos_in[2])
     pl.semaphore_wait(barrier, n_gy - 1 + has[0].astype(i32) + has[1].astype(i32))
     for m in order:
         label_copy(m).start()
@@ -257,17 +256,17 @@
     got_pos[:, part(gy), :] = send_pos[:, part(gy), :]
     inputs[4].wait()
     inputs[5].wait()
-    both = in_order(jnp.concatenate([vel_in[0], vel_in[1]], axis=1))
+    both = picked(chosen, jnp.concatenate([vel_in[0], vel_in[1]], axis=1))
     send_rest[0] = both[:, :128]
     send_rest[1] = both[:, 128:]
-    both = in_order(jnp.concatenate([vel_in[2], coef_in[pl.ds(0, elems, stride=2), :]], axis=1))
+    both = picked(chosen, jnp.concatenate([vel_in[2], coef_in[pl.ds(0, elems, stride=2), :]], axis=1))
     live = lax.dot_general(
         chosen, jnp.broadcast_to(count_in[...].astype(f32), (128, elems)).astype(bf16), across_lanes,
         preferred_element_type=f32,
     )
     send_rest[2] = both[:, :128]
     send_rest[3] = jnp.where(lane_iota((elems, 128)).astype(f32) < live, both[:, 128:], 0.0)
-    send_rest[4] = in_order(coef_in[pl.ds(1, elems, stride=2), :])
+    send_rest[4] = picked(chosen, coef_in[pl.ds(1, elems, stride=2), :])
     for m in range(1, near):
         rest_copy(m).start()
     got_rest[:, part(gy), :] = send_rest[:, part(gy), :]
@@ -281,6 +280,8 @@
     def within(i):
         return jnp.minimum(jnp.maximum(i, 0), elems - 1)
 
+    base = (0, elems - columns)
+
     def slot_of(e):
         return within(slot_s[0, e])
 
@@ -297,39 +298,69 @@
 
     slot_copy = pltpu.make_async_copy(slot_row, slot_s, tag_sem.at[n_gy])
 
+    def forces(start, count):
+        def some(i, carry):
+            m = lax.div(start + i * 8, share)
+            at = pl.ds(pl.multiple_of(partner(m) * share + lax.rem(start + i * 8, share), 8), 8)
+            rel = [fluid_ref[c, at, :] - got_rest[c, at, :] for c in range(3)]
+            speed = jnp.sqrt(rel[0] * rel[0] + rel[1] * rel[1] + rel[2] * rel[2])
+            power = jnp.exp(0.687 * jnp.log(got_rest[4, at, :] * speed))
+            factor = got_rest[3, at, :] * (1.0 + 0.15 * power)
+            for c in range(3):
+                drag_ref[c, at, :] = factor * rel[c]
+            return carry
+
+        lax.fori_loop(0, count // 8, some, 0)
+
+    def deposit_step(index, carry):
+        source = partner(lax.div(index, per))
+        first = lax.rem(index, per) * group
+        for u in range(group):
+            i = first + u
+            slot = source * share + i
+            layer = jnp.full((8, 128), tag_s[source, 0, gy * share + i], i32)
+            shift = jnp.where(layer < columns, -2.0 * WIDTH, 2.0 * WIDTH)
+            r, s, t = (wide_line(got_pos, d, slot) * WIDTH for d in range(3))
+            weights = (gauss(r, nodes), gauss(r + shift, nodes))
+            force = [-line(drag_ref, c, slot) for c in range(3)]
+            left = jnp.concatenate([f * w for w in weights for f in force], axis=0)
+            out = project(left, jnp.concatenate(st_planes(s, t, nodes), axis=1))
+            dep_ref[pl.ds(pl.multiple_of(slot * 2 * ROWS, 8), 2 * ROWS), 0:64] = out
+        return carry
+
     def interpolate(index, carry):
         @pl.when(index == per)
         def _():
+            forces(0, share)
+            lax.fori_loop(0, per, deposit_step, 0)
+            for m in range(near, n_gy):
+                pos_copy(m).wait_send()
+                rest_copy(m).start()
             for m in order:
                 label_copy(m).wait()
             total = got_label[0]
             for other in range(1, n_gy):
                 total = total + got_label[other]
-            slot_row[...] = total[:, 128:]
+            slot_row[...] = total[:, elems:]
             slot_copy.start()
             for m in order:
                 tag_copy(partner(m), m).start()
-            for m in range(near, n_gy):
-                pos_copy(m).wait_send()
-                rest_copy(m).start()
-            slot_copy.wait()
-            for m in order:
-                tag_copy(partner(m), m).wait()
-
-        for m in range(1, near):
-            @pl.when(index == m * per)
-            def _():
+            wanted = (turned(total[:, elems:]) == wide).astype(bf16)
+            for m in range(1, near):
                 pos_copy(m).wait()
-
-        @pl.when(index == near * per)
-        def _():
             for m in range(near, n_gy):
                 pos_copy(m).wait_recv()
-            collect(pos_ref, got_pos, 0, columns)
+            for c in range(3):
+                held = picked(wanted, got_pos[c])
+                for side in range(2):
+                    pos_ref[side, c] = held[base[side] : base[side] + columns]
             for side in range(2):
                 @pl.when(has[side])
                 def _():
                     to_side(side, pos_ref.at[side], gpos_ref.at[1 - side], pos_sem).start()
+            slot_copy.wait()
+            for m in order:
+                tag_copy(partner(m), m).wait()
 
         source = partner(lax.div(index, per))
         first = lax.rem(index, per) * group
@@ -356,22 +387,9 @@
 
     lax.fori_loop(0, elems // group, interpolate, 0)
 
-    def forces(start, count):
-        def some(i, carry):
-            m = lax.div(start + i * 8, share)
-            at = pl.ds(pl.multiple_of(partner(m) * share + lax.rem(start + i * 8, share), 8), 8)
-            rel = [fluid_ref[c, at, :] - got_rest[c, at, :] for c in range(3)]
-            speed = jnp.sqrt(rel[0] * rel[0] + rel[1] * rel[1] + rel[2] * rel[2])
-            power = jnp.exp(0.687 * jnp.log(got_rest[4, at, :] * speed))
-            factor = got_rest[3, at, :] * (1.0 + 0.15 * power)
-            for c in range(3):
-                drag_ref[c, at, :] = factor * rel[c]
-            return carry
-
-        lax.fori_loop(0, count // 8, some, 0)
-
     def strip(k):
-        return lax.rem(k * (eyd - 1), eyd)
+        odd = lax.rem(k, 2)
+        return odd * (eyd - 1) + (1 - 2 * odd) * lax.div(k, 2)
 
     def drag_copy(make, side, y):
         at = pl.ds(pl.multiple_of(y * ez, 8), ez)
@@ -381,20 +399,20 @@
         for side in range(2):
             @pl.when(has[side])
             def _():
-                drag_copy(to_side, side, k * (eyd - 1) % eyd).start()
+                drag_copy(to_side, side, strip(k)).start()
 
     def strip_sent(k):
         for side in range(2):
             @pl.when(has[side])
             def _():
-                drag_copy(to_side, side, k * (eyd - 1) % eyd).wait_send()
+                drag_copy(to_side, side, strip(k)).wait_send()
 
     def deposit(index, carry):
-        @pl.when(index == 0)
+        @pl.when(index == per)
         def _():
             for m in range(1, near):
                 rest_copy(m).wait()
-            forces(0, near * share)
+            forces(share, (near - 1) * share)
 
         @pl.when(index == near * per)
         def _():
@@ -402,28 +420,15 @@
                 rest_copy(m).wait()
             forces(near * share, elems - near * share)
             collect(out_ref, drag_ref, 0, columns)
-            for k in range(eyd):
+            for k in range(2):
                 strip_start(k)
             for m in order:
                 back_copy(m).start()
             ret_ref[:, part(gy), :] = drag_ref[:, part(gy), :]
 
-        source = partner(lax.div(index, per))
-        first = lax.rem(index, per) * group
-        for u in range(group):
-            i = first + u
-            slot = source * share + i
-            layer = jnp.full((8, 128), tag_s[source, 0, gy * share + i], i32)
-            shift = jnp.where(layer < columns, -2.0 * WIDTH, 2.0 * WIDTH)
-            r, s, t = (wide_line(got_pos, d, slot) * WIDTH for d in range(3))
-            weights = (gauss(r, nodes), gauss(r + shift, nodes))
-            force = [-line(drag_ref, c, slot) for c in range(3)]
-            left = jnp.concatenate([f * w for w in weights for f in force], axis=0)
-            out = project(left, jnp.concatenate(st_planes(s, t, nodes), axis=1))
-            dep_ref[pl.ds(pl.multiple_of(slot * 2 * ROWS, 8), 2 * ROWS), 0:64] = out
-        return carry
-
-    lax.fori_loop(0, elems // group, deposit, 0)
+        return deposit_step(index, carry)
+
+    lax.fori_loop(per, elems // group, deposit, 0)
 
     def gather(i, carry):
         for side in range(exd):
@@ -446,17 +451,28 @@
 
     lax.fori_loop(0, columns // 8, gather, 0)
 
-    base = (0, elems - columns)
-    low_h = lane_iota((half, 128)) < 64
-    for side in range(2):
-        node = 0 if side == 0 else 7
-        for c in range(3):
-            one = ts_ref[pl.ds(base[side] * ROWS + c * 8 + node, half, stride=ROWS), :]
-            two = ts_ref[pl.ds((base[side] + half) * ROWS + c * 8 + node, half, stride=ROWS), :]
-            face_ref[side, c] = jnp.where(low_h, one, pltpu.roll(two, 64, 1))
-        @pl.when(has[side])
-        def _():
-            to_side(side, face_ref.at[side], gface_ref.at[1 - side], face_sem).start()
+    low = lane_iota((ez, 128)) < 64
+    pairs = eyd // 2
+
+    def face_copy(make, side, at):
+        rows = pl.ds(pl.multiple_of(at * ez, 8), ez)
+        there = 1 - side if make is to_side else side
+        return make(side, face_ref.at[side, :, rows], gface_ref.at[there, :, rows], face_sem, at)
+
+    for at in range(pairs):
+        for side in range(2):
+            node = 0 if side == 0 else 7
+            for c in range(3):
+                one = ts_ref[pl.ds((base[side] + at * ez) * ROWS + c * 8 + node, ez, stride=ROWS), :]
+                two = ts_ref[pl.ds((base[side] + (eyd - 1 - at) * ez) * ROWS + c * 8 + node, ez, stride=ROWS), :]
+                face_ref[side, c, at * ez : (at + 1) * ez, :] = jnp.where(low, one, pltpu.roll(two, 64, 1))
+    for at in range(pairs):
+        for side in range(2):
+            @pl.when(has[side])
+            def _():
+                face_copy(to_side, side, at).start()
+    for k in range(2, eyd):
+        strip_start(k)
 
     for side in range(2):
         @pl.when(has[side])
@@ -481,10 +497,6 @@
             final_ref[c, pl.ds(at, 8), :] = rows_of([line(ret_ref, c, spot) for spot in spots])
         return carry
 
-    place_copy.wait()
-    for m in order:
-        back_copy(m).wait()
-    lax.fori_loop(0, elems // 8, pick, 0)
 
     def ghost(k, carry):
         y = strip(k)
@@ -506,14 +518,6 @@
             ts_ref[spot, 0:64] = value
         return carry
 
-    lax.fori_loop(0, eyd, ghost, 0)
-
-    for side in range(2):
-        @pl.when(has[side])
-        def _():
-            from_side(side, face_ref.at[side], gface_ref.at[side], face_sem).wait()
-
-    low = lane_iota((ez, 128)) < 64
     spot64 = lane_iota((ez, 128)) % 64
     depth = lax.broadcasted_iota(jnp.int32, (ez, 128), 0)
     up = (spot64 % 8 == 7) & (depth < ez - 1)
@@ -527,41 +531,48 @@
         device_id={"gy": gy + 1}, device_id_type=mesh_id,
     )
 
-    def assemble(k, carry):
+    def through(v):
+        nxt = pltpu.roll(pltpu.roll(v, ez - 1, 0), 7, 1)
+        prv = pltpu.roll(pltpu.roll(v, 1, 0), 121, 1)
+        return v + jnp.where(up, nxt, 0.0) + jnp.where(down, prv, 0.0)
+
+    def lanes(c, x, y, q):
+        start = (x * columns + y * ez) * ROWS + c * 8 + 2 * q
+        even = ts_ref[pl.ds(start, ez, stride=ROWS), :]
+        odd = ts_ref[pl.ds(start + 1, ez, stride=ROWS), :]
+        return jnp.where(low, even, pltpu.roll(odd, 64, 1))
+
+    def far(c, side, y, at, upper):
+        came = gface_ref[side, c, pl.ds(pl.multiple_of(at * ez, 8), ez), :]
+        turn = pltpu.roll(came, 64, 1)
+        came = jnp.where(low != upper, came, turn)
+        mine = fs_ref[side, c, pl.ds(pl.multiple_of(y * ez, 8), ez), :]
+        mine = jnp.where(low, mine, pltpu.roll(mine, 64, 1))
+        return jnp.where(has[side] & (low if side == 0 else jnp.logical_not(low)), came + mine, 0.0)
+
+    def assembled(k):
         y = strip(k)
-        upper = y >= eyd // 2
-
-        def lanes(c, x, q):
-            start = (x * columns + y * ez) * ROWS + c * 8 + 2 * q
-            even = ts_ref[pl.ds(start, ez, stride=ROWS), :]
-            odd = ts_ref[pl.ds(start + 1, ez, stride=ROWS), :]
-            return jnp.where(low, even, pltpu.roll(odd, 64, 1))
-
-        def far(c, side):
-            came = gface_ref[side, c, pl.ds(pl.multiple_of(lax.rem(y, eyd // 2) * ez, 8), ez), :]
-            turned = pltpu.roll(came, 64, 1)
-            came = jnp.where(low != upper, came, turned)
-            mine = fs_ref[side, c, pl.ds(pl.multiple_of(y * ez, 8), ez), :]
-            mine = jnp.where(low, mine, pltpu.roll(mine, 64, 1))
-            return jnp.where(has[side], came + mine, 0.0)
-
-        edges = []
+        out = []
         for c in range(3):
-            grid = [[lanes(c, x, q) for q in range(4)] for x in range(exd)]
+            grid = [[lanes(c, x, y, q) for q in range(4)] for x in range(exd)]
             for x in range(exd):
-                above = pltpu.roll(grid[x + 1][0], 64, 1) if x + 1 < exd else far(c, 1)
-                below = pltpu.roll(grid[x - 1][3], 64, 1) if x > 0 else far(c, 0)
                 done = list(grid[x])
-                done[3] = done[3] + jnp.where(low, 0.0, above)
-                done[0] = done[0] + jnp.where(low, below, 0.0)
-                for q in range(4):
-                    nxt = pltpu.roll(pltpu.roll(done[q], ez - 1, 0), 7, 1)
-                    prv = pltpu.roll(pltpu.roll(done[q], 1, 0), 121, 1)
-                    done[q] = done[q] + jnp.where(up, nxt, 0.0) + jnp.where(down, prv, 0.0)
+                if x + 1 < exd:
+                    done[3] = done[3] + jnp.where(low, 0.0, pltpu.roll(grid[x + 1][0], 64, 1))
+                else:
+                    done[3] = done[3] + far(c, 1, y, lax.div(k, 2), lax.rem(k, 2) == 1)
+                if x > 0:
+                    done[0] = done[0] + jnp.where(low, pltpu.roll(grid[x - 1][3], 64, 1), 0.0)
+                else:
+                    done[0] = done[0] + far(c, 0, y, lax.div(k, 2), lax.rem(k, 2) == 1)
+                done = [through(v) for v in done]
                 for q in range(4):
                     field_ref[c, x, y, :, q * 128 : (q + 1) * 128] = done[q]
-
-                edges.append((c, x, done))
+                out.append((c, x, done))
+        return out
+
+    def outer(k, carry):
+        edges = assembled(k)
 
         @pl.when(k == 0)
         def _():
@@ -589,7 +600,16 @@
 
         return carry
 
-    lax.fori_loop(0, eyd, assemble, 0)
+    def inner(k, carry):
+        ghost(k, carry)
+        assembled(k)
+        return carry
+
+    def above(v):
+        return jnp.where(spot64 >= 56, pltpu.roll(v, 56, 1), 0.0)
+
+    def below(v):
+        return jnp.where(spot64 < 8, pltpu.roll(v, 72, 1), 0.0)
 
     def across(c, carry):
         for x in range(exd):
@@ -599,15 +619,11 @@
                 for y in range(eyd):
                     v = cells[y]
                     if y + 1 < eyd:
-                        v = v + jnp.where(spot64 >= 56, pltpu.roll(cells[y + 1], 56, 1), 0.0)
+                        v = v + above(cells[y + 1])
                     if y > 0:
-                        v = v + jnp.where(spot64 < 8, pltpu.roll(cells[y - 1], 72, 1), 0.0)
+                        v = v + below(cells[y - 1])
                     field_ref[c, x, y, :, spot] = v
         return carry
-
-    lax.fori_loop(0, 3, across, 0)
-    for k in range(eyd):
-        strip_sent(k)
 
     def edge(far_ref, y, keep, turn):
         for c in range(3):
@@ -617,6 +633,26 @@
                     spot = slice(q * 128, (q + 1) * 128)
                     add = jnp.where(keep, pltpu.roll(far_edge, turn(q) % 128, 1), 0.0)
                     field_ref[c, x, y, :, spot] = field_ref[c, x, y, :, spot] + add
+
+    def face_wait(at):
+        for side in range(2):
+            @pl.when(has[side])
+            def _():
+                face_copy(from_side, side, at).wait()
+
+    lax.fori_loop(0, 2, ghost, 0)
+    place_copy.wait()
+    for m in order:
+        back_copy(m).wait()
+    lax.fori_loop(0, elems // 8, pick, 0)
+    face_wait(0)
+    lax.fori_loop(0, 2, outer, 0)
+    for at in range(1, pairs):
+        face_wait(at)
+    lax.fori_loop(2, eyd, inner, 0)
+    lax.fori_loop(0, 3, across, 0)
+    for k in range(eyd):
+        strip_sent(k)
 
     @pl.when(gy > 0)
     def _():
@@ -689,7 +725,7 @@
             dma((n_gy + 2,)),
             dma((2, 2)),
             dma((2, 2, eyd)),
-            dma((2, 2)),
+            dma((2, 2, eyd // 2)),
             dma((2, 2)),
             dma((2, n_gy - 1)),
         ],

time: 25.3 us -> 23.1 us (0.913)
  Pallas kernels: 24.5 us -> 22.3 us
    pallas_call x1, Pallas kernels: 23.6 us -> 21.3 us  [run_main(): pl.pallas_call(functools.partial(main_kernel, shape, n_gx, n_gy), out_sha...]
where the time goes in v5:
time: 23.1 us; the launch traced here: 22.9 us
  Pallas kernels  22.3 us (97%)
  between operations  0.64 us (3%)
    pallas_call x1, Pallas kernels, run_main(): pl.pallas_call(functools.partial(main_kernel, shape, n_gx, n_gy), out_sha...  21.3 us
    pallas_call x1, Pallas kernels, run_store(): pl.pallas_call(store_pass, out_shape=(jax.ShapeDtypeStruct(field.shape, f...  0.97 us

profile of v5, /device:TPU:9, one launch (start us, length us, event | category | flops | bytes accessed | tf_op | source)
XLA Modules:
  0.0 22.9 jit_solution(729801574107992511)
XLA Ops:
  0.6 21.3 %elements.1 = (f32[3,2,4,16,512]{4,3,2,1,0:T(8,128)S(1)}, f32[3,128,128]{2,1,0:T(8,128)S(1)}) custom-call(s32[1,128]{1,0:T(1,128)} %bitcast.12, s32[1,128]{1,0:T(1,128)} %bitcast.13, s32[1,128]{1,0:T(1,128)} %bitcast.14, f32[3,128,128]{2,1,0:T(8,128)} %bitcast.9, f32[3,128,128]{2,1,0:T(8,128)} %bitcast.10, f32[256,128]{1,0:T(8,128)} %bitcast.11, ...), custom_call_target="tpu_custom_call" | custom-call | tf_op jit(solution)/shard_map/elements/pallas_call | solution.py:681
  22.0 1.0 %store.1 = (f32[3,2,4,16,512]{4,3,2,1,0:T(8,128)}, f32[3,128,128]{2,1,0:T(8,128)}) custom-call(f32[3,2,4,16,512]{4,3,2,1,0:T(8,128)S(1)} %get-tuple-element.6.field_ref, f32[3,128,128]{2,1,0:T(8,128)S(1)} %get-tuple-element.7.final_ref), custom_call_target="tpu_custom_call" | custom-call | tf_op jit(solution)/shard_map/store/pallas_call | solution.py:750

commit v6 on v5

--- a/solution.py
+++ b/solution.py
@@ -189,6 +189,14 @@
 
     def tag_copy(index, m):
         return pltpu.make_async_copy(got_label.at[index], tag_s.at[index], tag_sem.at[m])
+
+    @pl.when(gy == 0)
+    def _():
+        far_hi_ref[...] = jnp.zeros(far_hi_ref.shape, jnp.float32)
+
+    @pl.when(gy == n_gy - 1)
+    def _():
+        far_lo_ref[...] = jnp.zeros(far_lo_ref.shape, jnp.float32)
 
     for side in range(2):
         @pl.when(jnp.logical_not(has[side]))
@@ -580,7 +588,7 @@
                 face = jnp.where(spot64 < 8, done[0], 0.0)
                 for q in range(1, 4):
                     face = face + pltpu.roll(jnp.where(spot64 < 8, done[q], 0.0), 8 * q, 1)
-                lo_ref[c, x] = face
+                lo_ref[c] = face if x == 0 else lo_ref[c] + pltpu.roll(face, 32 * x, 1)
 
             @pl.when(gy > 0)
             def _():
@@ -592,7 +600,7 @@
                 face = jnp.where(spot64 >= 56, done[0], 0.0)
                 for q in range(1, 4):
                     face = face + pltpu.roll(jnp.where(spot64 >= 56, done[q], 0.0), 128 - 8 * q, 1)
-                hi_ref[c, x] = face
+                hi_ref[c] = face if x == 0 else hi_ref[c] + pltpu.roll(face, 32 * x, 1)
 
             @pl.when(gy < n_gy - 1)
             def _():
@@ -625,14 +633,16 @@
                     field_ref[c, x, y, :, spot] = v
         return carry
 
-    def edge(far_ref, y, keep, turn):
-        for c in range(3):
-            for x in range(exd):
-                far_edge = far_ref[c, x]
-                for q in range(4):
-                    spot = slice(q * 128, (q + 1) * 128)
-                    add = jnp.where(keep, pltpu.roll(far_edge, turn(q) % 128, 1), 0.0)
-                    field_ref[c, x, y, :, spot] = field_ref[c, x, y, :, spot] + add
+    def edges_in(c, carry):
+        for x in range(exd):
+            hi, lo = far_hi_ref[c], far_lo_ref[c]
+            for q in range(4):
+                spot = slice(q * 128, (q + 1) * 128)
+                add = jnp.where(spot64 < 8, pltpu.roll(hi, (72 + 8 * q - 32 * x) % 128, 1), 0.0)
+                field_ref[c, x, 0, :, spot] = field_ref[c, x, 0, :, spot] + add
+                add = jnp.where(spot64 >= 56, pltpu.roll(lo, (56 - 8 * q - 32 * x) % 128, 1), 0.0)
+                field_ref[c, x, eyd - 1, :, spot] = field_ref[c, x, eyd - 1, :, spot] + add
+        return carry
 
     def face_wait(at):
         for side in range(2):
@@ -640,11 +650,11 @@
             def _():
                 face_copy(from_side, side, at).wait()
 
-    lax.fori_loop(0, 2, ghost, 0)
     place_copy.wait()
     for m in order:
         back_copy(m).wait()
     lax.fori_loop(0, elems // 8, pick, 0)
+    lax.fori_loop(0, 2, ghost, 0)
     face_wait(0)
     lax.fori_loop(0, 2, outer, 0)
     for at in range(1, pairs):
@@ -657,14 +667,14 @@
     @pl.when(gy > 0)
     def _():
         hi_copy.wait_recv()
-        edge(far_hi_ref, 0, spot64 < 8, lambda q: 72 + 8 * q)
         lo_copy.wait_send()
 
     @pl.when(gy < n_gy - 1)
     def _():
         lo_copy.wait_recv()
-        edge(far_lo_ref, eyd - 1, spot64 >= 56, lambda q: 56 - 8 * q)
         hi_copy.wait_send()
+
+    lax.fori_loop(0, 3, edges_in, 0)
 
 
 def run_main(arrays, shape):
@@ -674,7 +684,7 @@
     n_gx, n_gy = lax.axis_size("gx"), lax.axis_size("gy")
     f32, i32 = jnp.float32, jnp.int32
     dma = pltpu.SemaphoreType.DMA
-    face = (3, exd, ez, 128)
+    face = (3, ez, 128)
     label = (n_gy, 1, 2 * elems)
     strips = (2, 3, columns, 128)
     hbm = [pltpu.with_memory_space_constraint(x, pltpu.HBM) for x in arrays]

time: 23.1 us -> 23.1 us (level)
  no operation moved by 1% of the time
where the time goes in v6:
time: 23.1 us; the launch traced here: 22.9 us
  Pallas kernels  22.3 us (97%)
  between operations  0.64 us (3%)
    pallas_call x1, Pallas kernels, run_main(): pl.pallas_call(functools.partial(main_kernel, shape, n_gx, n_gy), out_sha...  21.3 us
    pallas_call x1, Pallas kernels, run_store(): pl.pallas_call(store_pass, out_shape=(jax.ShapeDtypeStruct(field.shape, f...  0.97 us

profile of v6, /device:TPU:9, one launch (start us, length us, event | category | flops | bytes accessed | tf_op | source)
XLA Modules:
  0.0 22.9 jit_solution(9422089862149541919)
XLA Ops:
  0.6 21.3 %elements.1 = (f32[3,2,4,16,512]{4,3,2,1,0:T(8,128)S(1)}, f32[3,128,128]{2,1,0:T(8,128)S(1)}) custom-call(s32[1,128]{1,0:T(1,128)} %bitcast.12, s32[1,128]{1,0:T(1,128)} %bitcast.13, s32[1,128]{1,0:T(1,128)} %bitcast.14, f32[3,128,128]{2,1,0:T(8,128)} %bitcast.9, f32[3,128,128]{2,1,0:T(8,128)} %bitcast.10, f32[256,128]{1,0:T(8,128)} %bitcast.11, ...), custom_call_target="tpu_custom_call" | custom-call | tf_op jit(solution)/shard_map/elements/pallas_call | solution.py:691
  21.9 1.0 %store.1 = (f32[3,2,4,16,512]{4,3,2,1,0:T(8,128)}, f32[3,128,128]{2,1,0:T(8,128)}) custom-call(f32[3,2,4,16,512]{4,3,2,1,0:T(8,128)S(1)} %get-tuple-element.6.field_ref, f32[3,128,128]{2,1,0:T(8,128)S(1)} %get-tuple-element.7.final_ref), custom_call_target="tpu_custom_call" | custom-call | tf_op jit(solution)/shard_map/store/pallas_call | solution.py:760
